TPU v7x, 256 devices: a whole 4x4x8 slice. The times are simulated.
256 devices in a mesh: ctg: 32 (over x, y, core), br: 8 (over z).
Axes of the slice: x: 4, y: 4, z: 8, core: 2. Of those that a mesh axis runs over, the one named last changes fastest.
Arguments:
- base_vm: float32 [10240], P(('ctg', 'br')), may hold values from 0.95 to 1.05
- base_va: float32 [10240], P(('ctg', 'br')), may hold values from -0.6 to 0.6
- delta_state: float32 [256, 2, 10240], P('ctg', None, 'br'), may hold values from -0.18 to 0.18
- multipliers: float32 [256, 2, 10240], P('ctg', None, 'br'), may hold values from -6 to 6
- net_inj: float32 [256, 2, 10240], P('ctg', None, 'br'), may hold values from -6 to 6
- ang_grad: float32 [256, 10240], P('ctg', 'br'), may hold values from -6 to 6
- from_bus: int32 [13312], P('br'), may hold values from 0 to 10239
- to_bus: int32 [13312], P('br'), may hold values from 0 to 10239
- status: int32 [256, 13312], P('ctg', 'br'), may hold values 0 or 1
- conduct: float32 [13312], P('br'), may hold values from 1 to 5
- suscept: float32 [13312], P('br'), may hold values from -15 to -5
- charging: float32 [13312], P('br'), may hold values from 0.1 to 0.6
- rating: float32 [13312], P('br'), may hold values from 1 to 3
- slack: float32 [256, 13312], P('ctg', 'br'), may hold values from 0.05 to 2
- zdual: float32 [256, 13312], P('ctg', 'br'), may hold values from 0.05 to 2
Outputs:
- mismatch: float32 [256, 2, 10240], P('ctg', None, 'br')
- dual_res: float32 [256, 10240], P('ctg', 'br')
- limit_res: float32 [256, 13312], P('ctg', 'br')
- ctg_norms: float32 [256, 4], P('ctg')
- total_norms: float32 [4], replicated
All inputs are finite; a program needn't handle non-finite values. No bound on the sum of `status` on one device may be relied on, other than what follows from the above.
Results may differ from a plain program's by a relative error of at most 0.0003.
Values sent between devices are 32-bit elements; how exact they have to be, the bound alone decides.
A program may use at most 64 MiB of HBM per device.

v0:
```python
import math

import jax
import jax.numpy as jnp
from jax import lax
from jax.sharding import PartitionSpec as P


def turned_gather(arrays, axis, dims):
    turned = [jnp.moveaxis(a, dim, 0) for a, dim in zip(arrays, dims)]
    widths = [t[0].size for t in turned]
    both = jnp.concatenate([t.reshape(-1, w) for t, w in zip(turned, widths)], axis=1)
    whole = lax.all_gather(both, axis, axis=0, tiled=True)
    pieces = jnp.split(whole, [sum(widths[:k]) for k in range(1, len(widths))], axis=1)
    return tuple(
        (
            jnp.moveaxis(b.reshape(-1, *t.shape[1:]), 0, dim)
            for b, t, dim in zip(pieces, turned, dims)
        )
    )


def in_one_piece(arrays, axis, dim, along):
    both = jnp.concatenate(arrays, axis=along)
    whole, at, finished = (lax.all_gather(both, axis, axis=dim, tiled=True), 0, [])
    for a in arrays:
        finished.append(lax.slice_in_dim(whole, at, at + a.shape[along], axis=along))
        at += a.shape[along]
    return tuple(finished)


def in_blocks(array, dim, peers):
    shape = array.shape
    pieces = array.reshape(*shape[:dim], peers, shape[dim] // peers, *shape[dim + 1 :])
    return jnp.moveaxis(pieces, dim, 0)


def summed_on_arrival(array, axis, dim):
    peers = lax.axis_size(axis)
    pieces = lax.all_to_all(in_blocks(array, dim, peers), axis, 0, 0, tiled=True)
    return jnp.sum(pieces, axis=0)


def sent_to_all(array, axis):
    copies = jnp.broadcast_to(array, (lax.axis_size(axis), *array.shape))
    return lax.all_to_all(copies, axis, split_axis=0, concat_axis=0, tiled=True)


def over_copies(array, axis):
    everything = sent_to_all(array, axis)
    return jnp.sum(everything, axis=0)


def in_one(arrays, axis):
    ends = [0]
    for a in arrays:
        ends.append(ends[-1] + a.size)
    subtotal = over_copies(jnp.concatenate([a.ravel() for a in arrays]), axis)
    return tuple((subtotal[b:e].reshape(a.shape) for a, b, e in zip(arrays, ends, ends[1:])))


def block_size(span_total, other_side):
    limit = max(128, (1 << 23) // other_side)
    power = 1 << limit.bit_length() - 1
    return math.gcd(span_total, min(1024, power))


def select_cols(values, index_list):
    row_count, bus_count = values.shape
    col_count = index_list.shape[0]
    span_cols = block_size(bus_count, col_count)
    block_count = bus_count // span_cols
    tiles = values.reshape(row_count, block_count, span_cols).transpose(1, 0, 2)

    def add_block(running, item):
        segment, number = item
        labels = number * span_cols + lax.iota(jnp.int32, span_cols)
        onehot = (labels[:, None] == index_list[None, :]).astype(jnp.float32)
        running = running + jnp.dot(
            segment, onehot, precision=lax.Precision.HIGHEST, preferred_element_type=jnp.float32
        )
        return (running, None)

    start_zero = jnp.zeros((row_count, col_count), jnp.float32)
    numbers = jnp.arange(block_count, dtype=jnp.int32)
    result, _ = lax.scan(add_block, start_zero, (tiles, numbers))
    return result


def spread_rows(values, index_list, bus_count):
    row_count, col_count = values.shape
    span_cols = block_size(bus_count, col_count)
    block_count = bus_count // span_cols

    def one_block(carry, number):
        labels = number * span_cols + lax.iota(jnp.int32, span_cols)
        onehot = (index_list[:, None] == labels[None, :]).astype(jnp.float32)
        piece_sum = jnp.dot(
            values, onehot, precision=lax.Precision.HIGHEST, preferred_element_type=jnp.float32
        )
        return (carry, piece_sum)

    numbers = jnp.arange(block_count, dtype=jnp.int32)
    _, pieces = lax.scan(one_block, jnp.int32(0), numbers)
    return pieces.transpose(1, 0, 2).reshape(row_count, bus_count)


def branch_flows(
    volt_mag, volt_ang, mult_p, mult_q, from_idx, to_idx, conduct, suscept, charging, in_service
):
    scen_count = volt_mag.shape[0]
    stacked = jnp.concatenate([volt_mag, volt_ang, mult_p, mult_q], 0)
    at_from_end = select_cols(stacked, from_idx)
    at_to_end = select_cols(stacked, to_idx)
    volt_from = at_from_end[:scen_count]
    volt_to = at_to_end[:scen_count]
    angle_diff = at_from_end[scen_count : 2 * scen_count] - at_to_end[scen_count : 2 * scen_count]
    mp_from = at_from_end[2 * scen_count : 3 * scen_count]
    mq_from = at_from_end[3 * scen_count :]
    mp_to = at_to_end[2 * scen_count : 3 * scen_count]
    mq_to = at_to_end[3 * scen_count :]
    cos_diff = jnp.cos(angle_diff)
    sin_diff = jnp.sin(angle_diff)
    volt_prod = volt_from * volt_to
    p_from = conduct * volt_from * volt_from - volt_prod * (conduct * cos_diff + suscept * sin_diff)
    q_from = -(suscept + charging) * volt_from * volt_from - volt_prod * (
        conduct * sin_diff - suscept * cos_diff
    )
    p_to = conduct * volt_to * volt_to - volt_prod * (conduct * cos_diff - suscept * sin_diff)
    q_to = -(suscept + charging) * volt_to * volt_to + volt_prod * (
        conduct * sin_diff + suscept * cos_diff
    )
    flow_dual = volt_prod * (
        mp_from * (conduct * sin_diff - suscept * cos_diff)
        - mq_from * (conduct * cos_diff + suscept * sin_diff)
        + mp_to * (conduct * sin_diff + suscept * cos_diff)
        + mq_to * (conduct * cos_diff - suscept * sin_diff)
    )
    at_from = jnp.stack([p_from, q_from, flow_dual], 1) * in_service[:, None, :]
    at_to = jnp.stack([p_to, q_to, -flow_dual], 1) * in_service[:, None, :]
    return (at_from, at_to)


def sum_at_buses(from_vals, to_vals, from_idx, to_idx, offset, bus_count):
    scen_count = from_vals.shape[0]
    both_vals = jnp.concatenate([from_vals, to_vals], 2).reshape(scen_count * 3, -1)
    both_idx = jnp.concatenate([from_idx, to_idx], 0) - offset
    summed = spread_rows(both_vals, both_idx, bus_count)
    return summed.reshape(scen_count, 3, bus_count)


def per_device(
    base_vm,
    base_va,
    delta_state,
    multipliers,
    net_inj,
    ang_grad,
    from_bus,
    to_bus,
    status,
    conduct,
    suscept,
    charging,
    rating,
    slack,
    zdual,
):
    full_vm, full_va = turned_gather((base_vm, base_va), ("ctg", "br"), (0, 0))
    shifts, duals_all = in_one_piece((delta_state, multipliers), "br", 2, 0)
    volt_mag = full_vm[None, :] + shifts[:, 0]
    volt_ang = full_va[None, :] + shifts[:, 1]
    in_service = status.astype(jnp.float32)
    at_from, at_to = branch_flows(
        volt_mag,
        volt_ang,
        duals_all[:, 0],
        duals_all[:, 1],
        from_bus,
        to_bus,
        conduct,
        suscept,
        charging,
        in_service,
    )
    limit_res = in_service * (
        at_from[:, 0] * at_from[:, 0] + at_from[:, 1] * at_from[:, 1] + slack - rating * rating
    )
    complement = in_service * (zdual * slack - 0.01)
    limit_part = jnp.sum(limit_res * limit_res, axis=1)
    comp_part = jnp.sum(complement * complement, axis=1)
    bus_terms = sum_at_buses(at_from, at_to, from_bus, to_bus, 0, shifts.shape[2])
    summed = summed_on_arrival(bus_terms, "br", 2)
    mismatch = summed[:, :2] - net_inj
    dual_res = summed[:, 2] + ang_grad
    mis_part = jnp.sum(mismatch * mismatch, axis=(1, 2))
    dual_part = jnp.sum(dual_res * dual_res, axis=1)
    mis_sq, dual_sq, limit_sq, comp_sq = in_one((mis_part, dual_part, limit_part, comp_part), "br")
    squares = jnp.stack([mis_sq, dual_sq, limit_sq, comp_sq], 1)
    ctg_norms = jnp.sqrt(squares)
    totals = over_copies(jnp.sum(squares, axis=0), "ctg")
    total_norms = jnp.sqrt(totals / (delta_state.shape[0] * lax.axis_size("ctg")))
    return (mismatch, dual_res, limit_res, ctg_norms, total_norms)


def solution(mesh):
    placed = (
        P(("ctg", "br")),
        P(("ctg", "br")),
        P("ctg", None, "br"),
        P("ctg", None, "br"),
        P("ctg", None, "br"),
        P("ctg", "br"),
        P("br"),
        P("br"),
        P("ctg", "br"),
        P("br"),
        P("br"),
        P("br"),
        P("br"),
        P("ctg", "br"),
        P("ctg", "br"),
    )
    return jax.shard_map(
        per_device,
        mesh=mesh,
        in_specs=placed,
        out_specs=(P("ctg", None, "br"), P("ctg", "br"), P("ctg", "br"), P("ctg", None), P()),
        check_vma=False,
    )
```

profile of v0, /device:TPU:1, one launch (start us, length us, event | category | flops | bytes accessed | tf_op | source)
XLA Modules:
  0.0 281.0 jit_solution(867481893369995764)
XLA Ops:
  10.5 67.2 %all-gather = f32[256,40,2]{1,2,0:T(2,128)S(1)} all-gather(f32[1,40,2]{1,2,0:T(2,128)S(1)} %maximum_bitcast_fusion.1), channel_id=1, replica_groups=mesh['ctg'=32,'br'=8] {'ctg','br'}, dimensions={0}, use_global_device_ids=true | all-gather | bytes 82240 | tf_op jit(solution)/shard_map/all_gather | solution.py:13
  79.9 36.7 %while.34 = (s32[]{:T(128)}, f32[32,1664]{1,0:T(8,128)S(1)}, f32[10,32,1024]{2,1,0:T(8,128)S(1)}, s32[10]{0:T(128)S(1)}, s32[1664]{0:T(1024)S(1)}, /*index=5*/s32[]{:T(128)}, s32[1]{0:T(128)}, s32[]{:T(128)}) while((s32[]{:T(128)}, f32[32,1664]{1,0:T(8,128)S(1)}, f32[10,32,1024]{2,1,0:T(8,128)S(1)}, s32[10]{0:T(128)S(1)}, ...), condition=%wide.region_3.4_spmd.clone, body=%wide.region_2.3_spmd.clone.sunk | while | flops 656122880 | bytes 573567 | solution.py:86
  84.8 2.4 fusion.71
  88.5 2.4 fusion.71
  92.2 2.4 fusion.71
  95.8 2.4 fusion.71
  99.5 2.4 fusion.71
  103.2 2.4 fusion.71
  106.9 2.4 fusion.71
  110.5 2.4 fusion.71
  114.2 2.4 fusion.71
  116.6 36.7 %while.33 = (s32[]{:T(128)}, f32[32,1664]{1,0:T(8,128)S(1)}, f32[10,32,1024]{2,1,0:T(8,128)S(1)}, s32[10]{0:T(128)S(1)}, s32[1664]{0:T(1024)S(1)}, /*index=5*/s32[]{:T(128)}, s32[1]{0:T(128)}, s32[]{:T(128)}) while((s32[]{:T(128)}, f32[32,1664]{1,0:T(8,128)S(1)}, f32[10,32,1024]{2,1,0:T(8,128)S(1)}, s32[10]{0:T(128)S(1)}, ...), condition=%wide.region_1.2_spmd.clone, body=%wide.region_0.1_spmd.clone.sunk | while | flops 656122880 | bytes 573567 | solution.py:86
  121.6 2.4 fusion.68
  125.2 2.4 fusion.68
  139.9 2.4 fusion.68
  143.6 2.4 fusion.68
  147.3 2.4 fusion.68
  154.0 59.3 %while.32 = (s32[]{:T(128)}, f32[10,24,1024]{2,1,0:T(8,128)}, s32[3328]{0:T(1024)S(1)}, s32[10]{0:T(128)S(1)}, f32[24,3328]{1,0:T(8,128)S(1)}, /*index=5*/s32[]{:T(128)}, s32[1]{0:T(128)}) while((s32[]{:T(128)}, f32[10,24,1024]{2,1,0:T(8,128)}, s32[3328]{0:T(1024)S(1)}, s32[10]{0:T(128)S(1)}, f32[24,3328]{1,0:T(8,128)S(1)}, ...), condition=%wide.region_5.6_spmd, body=%wide.region_4.5_spmd.sunk | while | flops 984876032 | bytes 439913 | solution.py:104
  155.3 4.7 %fusion.65 = f32[10,24,1024]{2,1,0:T(8,128)} fusion(f32[10,24,1024]{2,1,0:T(8,128)} %get-tuple-element.346, s32[]{:T(128)} %get-tuple-element.345, f32[24,3328]{1,0:T(8,128)S(1)} %get-tuple-element.356, s32[1024]{0:T(1024)S(1)} %iota_add_fusion.6, s32[3328]{0:T(1024)S(1)} %get-tuple-element.354), kind=kOutput, calls=%fused_computation.5.clone.1 | convolution fusion | flops 984875008 | bytes 435712 | tf_op jit(solution)/shard_map/while/body/eval_jaxpr/dot_general | solution.py:98
  161.2 4.7 %fusion.65 = f32[10,24,1024]{2,1,0:T(8,128)} fusion(f32[10,24,1024]{2,1,0:T(8,128)} %get-tuple-element.346, s32[]{:T(128)} %get-tuple-element.345, f32[24,3328]{1,0:T(8,128)S(1)} %get-tuple-element.356, s32[1024]{0:T(1024)S(1)} %iota_add_fusion.6, s32[3328]{0:T(1024)S(1)} %get-tuple-element.354), kind=kOutput, calls=%fused_computation.5.clone.1 | convolution fusion | flops 984875008 | bytes 435712 | tf_op jit(solution)/shard_map/while/body/eval_jaxpr/dot_general | solution.py:98
  167.2 4.7 %fusion.65 = f32[10,24,1024]{2,1,0:T(8,128)} fusion(f32[10,24,1024]{2,1,0:T(8,128)} %get-tuple-element.346, s32[]{:T(128)} %get-tuple-element.345, f32[24,3328]{1,0:T(8,128)S(1)} %get-tuple-element.356, s32[1024]{0:T(1024)S(1)} %iota_add_fusion.6, s32[3328]{0:T(1024)S(1)} %get-tuple-element.354), kind=kOutput, calls=%fused_computation.5.clone.1 | convolution fusion | flops 984875008 | bytes 435712 | tf_op jit(solution)/shard_map/while/body/eval_jaxpr/dot_general | solution.py:98
  173.1 4.7 %fusion.65 = f32[10,24,1024]{2,1,0:T(8,128)} fusion(f32[10,24,1024]{2,1,0:T(8,128)} %get-tuple-element.346, s32[]{:T(128)} %get-tuple-element.345, f32[24,3328]{1,0:T(8,128)S(1)} %get-tuple-element.356, s32[1024]{0:T(1024)S(1)} %iota_add_fusion.6, s32[3328]{0:T(1024)S(1)} %get-tuple-element.354), kind=kOutput, calls=%fused_computation.5.clone.1 | convolution fusion | flops 984875008 | bytes 435712 | tf_op jit(solution)/shard_map/while/body/eval_jaxpr/dot_general | solution.py:98
  179.0 4.7 %fusion.65 = f32[10,24,1024]{2,1,0:T(8,128)} fusion(f32[10,24,1024]{2,1,0:T(8,128)} %get-tuple-element.346, s32[]{:T(128)} %get-tuple-element.345, f32[24,3328]{1,0:T(8,128)S(1)} %get-tuple-element.356, s32[1024]{0:T(1024)S(1)} %iota_add_fusion.6, s32[3328]{0:T(1024)S(1)} %get-tuple-element.354), kind=kOutput, calls=%fused_computation.5.clone.1 | convolution fusion | flops 984875008 | bytes 435712 | tf_op jit(solution)/shard_map/while/body/eval_jaxpr/dot_general | solution.py:98
  184.9 4.7 %fusion.65 = f32[10,24,1024]{2,1,0:T(8,128)} fusion(f32[10,24,1024]{2,1,0:T(8,128)} %get-tuple-element.346, s32[]{:T(128)} %get-tuple-element.345, f32[24,3328]{1,0:T(8,128)S(1)} %get-tuple-element.356, s32[1024]{0:T(1024)S(1)} %iota_add_fusion.6, s32[3328]{0:T(1024)S(1)} %get-tuple-element.354), kind=kOutput, calls=%fused_computation.5.clone.1 | convolution fusion | flops 984875008 | bytes 435712 | tf_op jit(solution)/shard_map/while/body/eval_jaxpr/dot_general | solution.py:98
  190.9 4.7 %fusion.65 = f32[10,24,1024]{2,1,0:T(8,128)} fusion(f32[10,24,1024]{2,1,0:T(8,128)} %get-tuple-element.346, s32[]{:T(128)} %get-tuple-element.345, f32[24,3328]{1,0:T(8,128)S(1)} %get-tuple-element.356, s32[1024]{0:T(1024)S(1)} %iota_add_fusion.6, s32[3328]{0:T(1024)S(1)} %get-tuple-element.354), kind=kOutput, calls=%fused_computation.5.clone.1 | convolution fusion | flops 984875008 | bytes 435712 | tf_op jit(solution)/shard_map/while/body/eval_jaxpr/dot_general | solution.py:98
  196.8 4.7 %fusion.65 = f32[10,24,1024]{2,1,0:T(8,128)} fusion(f32[10,24,1024]{2,1,0:T(8,128)} %get-tuple-element.346, s32[]{:T(128)} %get-tuple-element.345, f32[24,3328]{1,0:T(8,128)S(1)} %get-tuple-element.356, s32[1024]{0:T(1024)S(1)} %iota_add_fusion.6, s32[3328]{0:T(1024)S(1)} %get-tuple-element.354), kind=kOutput, calls=%fused_computation.5.clone.1 | convolution fusion | flops 984875008 | bytes 435712 | tf_op jit(solution)/shard_map/while/body/eval_jaxpr/dot_general | solution.py:98
  202.7 4.7 %fusion.65 = f32[10,24,1024]{2,1,0:T(8,128)} fusion(f32[10,24,1024]{2,1,0:T(8,128)} %get-tuple-element.346, s32[]{:T(128)} %get-tuple-element.345, f32[24,3328]{1,0:T(8,128)S(1)} %get-tuple-element.356, s32[1024]{0:T(1024)S(1)} %iota_add_fusion.6, s32[3328]{0:T(1024)S(1)} %get-tuple-element.354), kind=kOutput, calls=%fused_computation.5.clone.1 | convolution fusion | flops 984875008 | bytes 435712 | tf_op jit(solution)/shard_map/while/body/eval_jaxpr/dot_general | solution.py:98
  208.7 4.7 %fusion.65 = f32[10,24,1024]{2,1,0:T(8,128)} fusion(f32[10,24,1024]{2,1,0:T(8,128)} %get-tuple-element.346, s32[]{:T(128)} %get-tuple-element.345, f32[24,3328]{1,0:T(8,128)S(1)} %get-tuple-element.356, s32[1024]{0:T(1024)S(1)} %iota_add_fusion.6, s32[3328]{0:T(1024)S(1)} %get-tuple-element.354), kind=kOutput, calls=%fused_computation.5.clone.1 | convolution fusion | flops 984875008 | bytes 435712 | tf_op jit(solution)/shard_map/while/body/eval_jaxpr/dot_general | solution.py:98
  216.6 4.0 %all-to-all-start = ((f32[8,8,3,1280]{3,1,2,0:T(8,128)}), f32[8,8,3,1280]{3,1,2,0:T(8,128)S(1)}, u32[]{:S(2)}, u32[]{:S(2)}) async-start(f32[8,8,3,1280]{3,1,2,0:T(8,128)} %copy.60), calls=%async_computation | async-start | bytes 1966080 | tf_op jit(solution)/shard_map/all_to_all | solution.py:40
  221.5 24.0 %all-to-all-done = f32[8,8,3,1280]{3,1,2,0:T(8,128)S(1)} async-done(((f32[8,8,3,1280]{3,1,2,0:T(8,128)}), f32[8,8,3,1280]{3,1,2,0:T(8,128)S(1)}, u32[]{:S(2)}, u32[]{:S(2)}) %all-to-all-start) | async-done | bytes 983072 | tf_op jit(solution)/shard_map/all_to_all | solution.py:40
  247.1 8.9 %all_to_all.17 = f32[8,1,32]{2,1,0:T(1,128)S(1)} all-to-all(f32[8,1,32]{2,1,0:T(1,128)S(1)} %broadcast_in_dim.14), channel_id=1, replica_groups=mesh['ctg'=32,'br'=8] {'br'}, dimensions={0} | all-to-all | bytes 2048 | tf_op jit(solution)/shard_map/all_to_all | solution.py:46
  256.9 16.7 %all_to_all.18 = f32[32,1,4]{2,1,0:T(1,128)S(1)} all-to-all(f32[32,1,4]{2,1,0:T(1,128)S(1)} %broadcast_in_dim.15), channel_id=1, replica_groups=mesh['ctg'=32,'br'=8] {'ctg'}, dimensions={0} | all-to-all | bytes 1024 | tf_op jit(solution)/shard_map/all_to_all | solution.py:46
  (137 shorter events, 45.0 us)
Async XLA Ops:
  7.2 71.0 %copy-start = (s32[8,1664]{1,0:T(8,128)S(1)}, s32[8,1664]{1,0:T(8,128)}, u32[]{:S(2)}) copy-start(s32[8,1664]{1,0:T(8,128)} %param.29) | copy-start | bytes 159748
  7.2 71.0 %copy-start.9 = (s32[1664]{0:T(1024)S(1)}, s32[1664]{0:T(1024)}, u32[]{:S(2)}) copy-start(s32[1664]{0:T(1024)} %param.28) | copy-start | bytes 19972
  7.2 71.0 %copy-start.10 = (s32[1664]{0:T(1024)S(1)}, s32[1664]{0:T(1024)}, u32[]{:S(2)}) copy-start(s32[1664]{0:T(1024)} %param.27) | copy-start | bytes 19972
  7.2 71.0 %copy-start.2 = (f32[1664]{0:T(1024)S(1)}, f32[1664]{0:T(1024)}, u32[]{:S(2)}) copy-start(f32[1664]{0:T(1024)} %param.31) | copy-start | bytes 19972
  7.2 71.0 %copy-start.8 = (f32[1664]{0:T(1024)S(1)}, f32[1664]{0:T(1024)}, u32[]{:S(2)}) copy-start(f32[1664]{0:T(1024)} %param.32) | copy-start | bytes 19972
  7.2 71.0 %all-gather.3.cloned.1.call-start = ((), (), s32[]{:S(2)}) async-start(), calls=%async_computation.3 | async-start | bytes 1474560 | tf_op jit(solution)/shard_map/all_gather | solution.py:25
  116.6 36.7 %copy-start.6 = (f32[1664]{0:T(1024)S(1)}, f32[1664]{0:T(1024)}, u32[]{:S(2)}) copy-start(f32[1664]{0:T(1024)} %param.30) | copy-start | bytes 19972
  216.6 4.0 %copy-start.7 = (f32[1664]{0:T(1024)S(1)}, f32[1664]{0:T(1024)}, u32[]{:S(2)}) copy-start(f32[1664]{0:T(1024)} %param.33) | copy-start | bytes 19972
  216.6 4.1 %copy-start.3 = (f32[8,1664]{1,0:T(8,128)S(1)}, f32[8,1664]{1,0:T(8,128)}, u32[]{:S(2)}) copy-start(f32[8,1664]{1,0:T(8,128)} %param.34) | copy-start | bytes 159748
  216.6 4.1 %copy-start.4 = (f32[8,1664]{1,0:T(8,128)S(1)}, f32[8,1664]{1,0:T(8,128)}, u32[]{:S(2)}) copy-start(f32[8,1664]{1,0:T(8,128)} %param.35) | copy-start | bytes 159748
  216.6 29.0 %copy-start.5 = (f32[8,1280]{1,0:T(8,128)S(1)}, f32[8,1280]{1,0:T(8,128)}, u32[]{:S(2)}) copy-start(f32[8,1280]{1,0:T(8,128)} %param.26) | copy-start | bytes 122884
  216.6 28.9 %all-to-all-start = ((f32[8,8,3,1280]{3,1,2,0:T(8,128)}), f32[8,8,3,1280]{3,1,2,0:T(8,128)S(1)}, u32[]{:S(2)}, u32[]{:S(2)}) async-start(f32[8,8,3,1280]{3,1,2,0:T(8,128)} %copy.60), calls=%async_computation | async-start | bytes 1966080 | tf_op jit(solution)/shard_map/all_to_all | solution.py:40
  220.7 25.7 %copy-start.1 = (f32[8,2,1280]{2,1,0:T(2,128)S(1)}, f32[8,2,1280]{2,1,0:T(2,128)}, u32[]{:S(2)}) copy-start(f32[8,2,1280]{2,1,0:T(2,128)} %param.25) | copy-start | bytes 245764
Sparse Core Ops, SparseCore 0:
  9.9 38.6 all-gather.2
where the time goes:
time: 283 us; the launch traced here: 281 us
  matrix products  94.7 us (33%)
  blocking collectives  92.8 us (33%)
  local copies, waits for them, and re-layouts  24.9 us (9%)
  waiting for transfers between devices  24.1 us (9%)
  loops' own time  20.3 us (7%)
  between operations  14.4 us (5%)
  other arithmetic  5.73 us (2%)
  starting transfers between devices  4.05 us (1%)
    all_gather x1, blocking collectives, turned_gather(): whole = lax.all_gather(both, axis, axis=0, tiled=True)  67.2 us
    dot_general x20, matrix products, add_block(): jnp.dot(segment, onehot, precision=lax.Precision.HIGHEST, preferred_eleme...  47.9 us
    dot_general x10, matrix products, one_block(): jnp.dot(values, onehot, precision=lax.Precision.HIGHEST, preferred_elemen...  46.8 us
    all_to_all x2, blocking collectives, sent_to_all(): return lax.all_to_all(copies, axis, split_axis=0, concat_axis=0, tiled=True)  25.6 us
    all_to_all x1, waiting for transfers between devices, summed_on_arrival(): lax.all_to_all(in_blocks(array, dim, peers), axis, 0, 0, tiled=True)  24 us
    dynamic_slice x30, local copies, waits for them, and re-layouts, select_cols(): result, _ = lax.scan(add_block, start_zero, (tiles, numbers))  17.6 us
    another operation x2, loops' own time, select_cols(): result, _ = lax.scan(add_block, start_zero, (tiles, numbers))  13.7 us
    another operation x1, loops' own time, spread_rows(): _, pieces = lax.scan(one_block, jnp.int32(0), numbers)  6.61 us
  transfers between devices with their start and end apart: 2, of which 1 were waited for; matrix products, arithmetic and copies ran while one was open for 1% of the time, Pallas kernels for 0%

commit v1 on v0

v1 whole, which is shorter than its diff:
```python
import functools

import jax
import jax.numpy as jnp
from jax import lax
from jax.experimental import pallas as pl
from jax.experimental.pallas import tpu as pltpu
from jax.sharding import PartitionSpec as P

F32, I32, BF16 = jnp.float32, jnp.int32, jnp.bfloat16
LANES = 128
MESH = pl.DeviceIdType.MESH


def kernel(
    planes,
    ranks,
    consts,
    delta,
    mult,
    net,
    ang,
    status,
    slack,
    zdual,
    mismatch,
    dual,
    limit,
    norms,
    total,
    consts_v,
    delta_v,
    mult_v,
    net_v,
    ang_v,
    status_v,
    slack_v,
    zdual_v,
    base_z,
    base_all,
    idx_f,
    coef,
    mult_all,
    delta_all,
    net_all,
    ang_all,
    status_all,
    slack_all,
    zdual_all,
    idx,
    tables,
    ends,
    terms,
    sums,
    mis_out,
    dual_out,
    limit_out,
    sq_mine,
    sq_all,
    tot_mine,
    tot_all,
    load_sem,
    send_sem,
    recv_sem,
    base_send,
    base_recv,
    tot_send,
    tot_recv,
):
    me = lax.axis_index("ctg")
    rank = lax.axis_index("br")
    nbus = delta.shape[2]
    nline = status.shape[1]
    bus_tiles, line_tiles = nbus // LANES, nline // LANES

    loads = [
        pltpu.make_async_copy(a, b, load_sem.at[n])
        for n, (a, b) in enumerate(
            (
                (consts, consts_v),
                (mult, mult_v),
                (delta, delta_v),
                (status, status_v),
                (slack, slack_v),
                (zdual, zdual_v),
                (net, net_v),
                (ang, ang_v),
            )
        )
    ]
    for c in loads:
        c.start()

    barrier = pltpu.get_barrier_semaphore()
    for d in range(1, ranks):
        pl.semaphore_signal(barrier, 1, device_id=(me, lax.rem(rank + d, ranks)), device_id_type=MESH)

    def greet(d, carry):
        pl.semaphore_signal(barrier, 1, device_id=(lax.rem(me + d, planes), rank), device_id_type=MESH)
        return carry

    lax.fori_loop(1, planes, greet, 0)
    for c in loads:
        c.wait()
    pl.semaphore_wait(barrier, ranks - 1 + planes - 1)

    groups = (
        (lambda s: consts_v.at[6:8, 0:LANES], lambda r: base_z.at[r], base_z),
        (lambda s: consts_v.at[0:2, :], lambda r: idx_f.at[:, r, :], idx_f),
        (lambda s: mult_v.at[s], lambda r: mult_all.at[:, r, :], mult_all),
        (lambda s: delta_v.at[s], lambda r: delta_all.at[:, r, :], delta_all),
        (lambda s: consts_v.at[2:6, :], lambda r: coef.at[:, r, :], coef),
        (lambda s: status_v.at[s], lambda r: status_all.at[r], status_all),
        (lambda s: slack_v.at[s], lambda r: slack_all.at[r], slack_all),
        (lambda s: zdual_v.at[s], lambda r: zdual_all.at[r], zdual_all),
        (lambda s: net_v.at[s], lambda r: net_all.at[:, r, :], net_all),
        (lambda s: ang_v.at[s], lambda r: ang_all.at[r], ang_all),
    )

    def send(n, source, place):
        pltpu.make_async_copy(source(rank), place(rank), recv_sem.at[n]).start()
        for d in range(1, ranks):
            peer = lax.rem(rank + d, ranks)
            pltpu.make_async_remote_copy(
                src_ref=source(peer),
                dst_ref=place(rank),
                send_sem=send_sem.at[n],
                recv_sem=recv_sem.at[n],
                device_id=(me, peer),
                device_id_type=MESH,
            ).start()

    def take(n, whole):
        pltpu.make_async_copy(whole, whole, recv_sem.at[n]).wait()

    for n, (source, place, _) in enumerate(groups):
        send(n, source, place)

    take(0, base_z)
    pltpu.make_async_copy(base_z, base_all.at[me], base_recv).start()

    def spread(d, carry):
        pltpu.make_async_remote_copy(
            src_ref=base_z,
            dst_ref=base_all.at[me],
            send_sem=base_send,
            recv_sem=base_recv,
            device_id=(lax.rem(me + d, planes), rank),
            device_id_type=MESH,
        ).start()
        return carry

    lax.fori_loop(1, planes, spread, 0)

    take(1, idx_f)
    idx[...] = idx_f[...].astype(I32)
    take(2, mult_all)
    tables[2:4] = mult_all[...]
    take(3, delta_all)
    pltpu.make_async_copy(base_all, base_all, base_recv).wait()
    piece = ranks * nbus // (planes * ranks)
    per_rank = nbus // piece
    group = planes // ranks
    for q in range(2):
        tiles = [jnp.zeros((ranks, LANES), F32) for _ in range(bus_tiles)]
        lane = lax.broadcasted_iota(I32, (ranks, LANES), 1)
        for p in range(per_rank):
            rows = jnp.concatenate(
                [base_all[r * group + p // ranks, p % ranks, q : q + 1, :] for r in range(ranks)], 0
            )
            first = p * piece
            t, off = first // LANES, first % LANES
            moved = pltpu.roll(rows, off, 1) if off else rows
            tiles[t] = jnp.where((lane >= off) & (lane < off + piece), moved, tiles[t])
            if off + piece > LANES:
                tiles[t + 1] = jnp.where(lane < off + piece - LANES, moved, tiles[t + 1])
        for t in range(bus_tiles):
            cols = slice(t * LANES, (t + 1) * LANES)
            tables[q, :, cols] = tiles[t] + delta_all[q, :, cols]

    def gather(k, carry):
        cols = pl.ds(pl.multiple_of(k * LANES, LANES), LANES)
        for e in range(2):
            where_to = idx[e, :, cols]
            high, low = where_to >> 7, where_to & 127
            found = [jnp.zeros((ranks, LANES), F32) for _ in range(4)]
            for h in range(ranks * bus_tiles):
                here = high == h
                r, t = h // bus_tiles, h % bus_tiles
                for q in range(4):
                    row = jnp.broadcast_to(
                        tables[q, r : r + 1, t * LANES : (t + 1) * LANES], (ranks, LANES)
                    )
                    got = jnp.take_along_axis(row, low, axis=1, mode="promise_in_bounds")
                    found[q] = jnp.where(here, got, found[q])
            for q in range(4):
                ends[4 * e + q, :, cols] = found[q]
        return carry

    lax.fori_loop(0, line_tiles, gather, 0)

    take(4, coef)
    take(5, status_all)
    take(6, slack_all)
    take(7, zdual_all)

    def flows(k, carry):
        limit_sq, comp_sq = carry
        cols = pl.ds(pl.multiple_of(k * LANES, LANES), LANES)
        vf, af, mpf, mqf = (ends[q, :, cols] for q in range(4))
        vt, at, mpt, mqt = (ends[4 + q, :, cols] for q in range(4))
        g, b, h, rating = (coef[q, :, cols] for q in range(4))
        live = status_all[:, cols].astype(F32)
        diff = af - at
        cs, sn = jnp.cos(diff), jnp.sin(diff)
        u = vf * vt
        gcs, gsn, bcs, bsn = g * cs, g * sn, b * cs, b * sn
        pf = (g * vf * vf - u * (gcs + bsn)) * live
        qf = (-(b + h) * vf * vf - u * (gsn - bcs)) * live
        pt = (g * vt * vt - u * (gcs - bsn)) * live
        qt = (-(b + h) * vt * vt + u * (gsn + bcs)) * live
        fd = u * (mpf * (gsn - bcs) - mqf * (gcs + bsn) + mpt * (gsn + bcs) + mqt * (gcs - bsn)) * live
        terms[0, :, cols] = pf
        terms[1, :, cols] = qf
        terms[2, :, cols] = fd
        terms[3, :, cols] = pt
        terms[4, :, cols] = qt
        terms[5, :, cols] = -fd
        sl = slack_all[:, cols]
        lim = live * (pf * pf + qf * qf + sl - rating * rating)
        limit_out[:, cols] = lim
        comp = live * (zdual_all[:, cols] * sl - 0.01)
        return limit_sq + lim * lim, comp_sq + comp * comp

    zero_tile = jnp.zeros((ranks, LANES), F32)
    limit_sq, comp_sq = lax.fori_loop(0, line_tiles, flows, (zero_tile, zero_tile))

    n_limit, n_mis, n_dual, n_sq = len(groups), len(groups) + 1, len(groups) + 2, len(groups) + 3
    send(n_limit, lambda s: limit_out.at[s], lambda r: limit.at[r])

    row16 = lax.broadcasted_iota(I32, (16, LANES), 0)
    per = nbus // 256
    high_of = [((row16 & 7) * per + j).astype(F32).astype(BF16) for j in range(per)]
    low_of = row16.astype(F32).astype(BF16)
    none16, one16 = jnp.zeros((16, LANES), BF16), jnp.ones((16, LANES), BF16)
    sums[...] = jnp.zeros_like(sums)

    def scatter(k, carry):
        cols = pl.ds(pl.multiple_of(k * LANES, LANES), LANES)
        for s in range(ranks):
            left, right = [], []
            for e in range(2):
                at_bus = idx[e, s : s + 1, cols]
                high = jnp.broadcast_to((at_bus >> 8).astype(F32), (16, LANES)).astype(BF16)
                low = jnp.broadcast_to((at_bus & 255).astype(F32), (16, LANES)).astype(BF16)
                vals = []
                for r in range(3):
                    v = terms[3 * e + r, s : s + 1, cols]
                    coarse = v.astype(BF16).astype(F32)
                    fine = v - coarse
                    vals.append(
                        jnp.concatenate(
                            [jnp.broadcast_to(coarse, (8, LANES)), jnp.broadcast_to(fine, (8, LANES))], 0
                        ).astype(BF16)
                    )
                rows = []
                for j in range(per):
                    here = high == high_of[j]
                    rows += [jnp.where(here, v, none16) for v in vals]
                left.append(jnp.concatenate(rows, 0))
                right.append(
                    jnp.concatenate(
                        [jnp.where(low == low_of + BF16(16 * t), one16, none16) for t in range(16)], 0
                    )
                )
            sums[...] += lax.dot_general(
                jnp.concatenate(left, 1),
                jnp.concatenate(right, 1),
                (((1,), (1,)), ((), ())),
                preferred_element_type=F32,
            )
        return carry

    lax.fori_loop(0, line_tiles, scatter, 0)

    take(8, net_all)
    take(9, ang_all)
    mis_sq, dual_sq = jnp.zeros((ranks, 256), F32), jnp.zeros((ranks, 256), F32)
    for j in range(per):
        cols = slice(256 * j, 256 * (j + 1))
        for r in range(3):
            first = (3 * j + r) * 16
            got = sums[first : first + 8, :] + sums[first + 8 : first + 16, :]
            if r < 2:
                out = got - net_all[r, :, cols]
                mis_out[r, :, cols] = out
                mis_sq += out * out
            else:
                out = got + ang_all[:, cols]
                dual_out[:, cols] = out
                dual_sq += out * out

    parts = [mis_sq, dual_sq, limit_sq, comp_sq]
    lane8 = lax.broadcasted_iota(I32, (1, LANES), 1)
    mine = jnp.zeros((1, LANES), F32)
    for n, part in enumerate(parts):
        mine = jnp.where(lane8 == n, jnp.sum(part, keepdims=True), mine)
    sq_mine[...] = mine
    send(n_sq, lambda s: sq_mine, lambda r: sq_all.at[r])
    send(n_mis, lambda s: mis_out.at[:, s, :], lambda r: mismatch.at[r])
    send(n_dual, lambda s: dual_out.at[s], lambda r: dual.at[r])

    take(n_sq, sq_all)
    squares = sq_all[:, 0, :]
    norms[...] = jnp.sqrt(squares)[:, 0:4]
    tot_mine[...] = jnp.sum(squares, axis=0, keepdims=True)
    pltpu.make_async_copy(tot_mine, tot_all.at[me], tot_recv).start()

    def share(d, carry):
        pltpu.make_async_remote_copy(
            src_ref=tot_mine,
            dst_ref=tot_all.at[me],
            send_sem=tot_send,
            recv_sem=tot_recv,
            device_id=(lax.rem(me + d, planes), rank),
            device_id_type=MESH,
        ).start()
        return carry

    lax.fori_loop(1, planes, share, 0)
    pltpu.make_async_copy(tot_all, tot_all, tot_recv).wait()
    whole = jnp.sum(tot_all[:, 0, :], axis=0, keepdims=True)
    total[...] = jnp.sqrt(whole / (planes * ranks))

    take(n_limit, limit)
    take(n_mis, mismatch)
    take(n_dual, dual)
    for n, (_, _, dest) in enumerate(groups):
        sent(send_sem.at[n], dest, ranks)
    for n, dest in ((n_limit, limit), (n_mis, mismatch), (n_dual, dual), (n_sq, sq_all)):
        sent(send_sem.at[n], dest, ranks)
    part = base_all.at[0 : planes - 1]
    pltpu.make_async_copy(part, part, base_send).wait()
    part = tot_all.at[0 : planes - 1]
    pltpu.make_async_copy(part, part, tot_send).wait()


def sent(sem, dest, ranks):
    dim = dest.shape.index(ranks)
    part = dest.at[(slice(None),) * dim + (slice(0, ranks - 1),)]
    pltpu.make_async_copy(part, part, sem).wait()


def per_device(
    base_vm,
    base_va,
    delta_state,
    multipliers,
    net_inj,
    ang_grad,
    from_bus,
    to_bus,
    status,
    conduct,
    suscept,
    charging,
    rating,
    slack,
    zdual,
):
    planes, ranks = lax.axis_size("ctg"), lax.axis_size("br")
    nscen, _, nbus = delta_state.shape
    nline = status.shape[1]
    widen = lambda a: jnp.pad(a, (0, nline - a.shape[0]))
    consts = jnp.stack(
        [
            from_bus.astype(F32),
            to_bus.astype(F32),
            conduct,
            suscept,
            charging,
            rating,
            widen(base_vm),
            widen(base_va),
        ]
    )
    hbm = pl.BlockSpec(memory_space=pl.ANY)
    vmem = pl.BlockSpec(memory_space=pltpu.VMEM)
    V = pltpu.VMEM
    bus, line = (ranks, nbus), (ranks, nline)
    sem = pltpu.SemaphoreType.DMA
    n_groups = 14
    mismatch, dual_res, limit_res, norms, total = pl.pallas_call(
        functools.partial(kernel, planes, ranks),
        out_shape=(
            jax.ShapeDtypeStruct((nscen, 2, nbus), F32),
            jax.ShapeDtypeStruct((nscen, nbus), F32),
            jax.ShapeDtypeStruct((nscen, nline), F32),
            jax.ShapeDtypeStruct((nscen, 4), F32),
            jax.ShapeDtypeStruct((1, LANES), F32),
        ),
        in_specs=[hbm] * 8,
        out_specs=(hbm, hbm, hbm, vmem, vmem),
        scratch_shapes=[
            V((8, nline), F32),
            V((nscen, 2, nbus), F32),
            V((nscen, 2, nbus), F32),
            V((nscen, 2, nbus), F32),
            V((nscen, nbus), F32),
            V((nscen, nline), I32),
            V((nscen, nline), F32),
            V((nscen, nline), F32),
            V((ranks, 2, LANES), F32),
            V((planes, ranks, 2, LANES), F32),
            V((2,) + line, F32),
            V((4,) + line, F32),
            V((2,) + bus, F32),
            V((2,) + bus, F32),
            V((2,) + bus, F32),
            V(bus, F32),
            V(line, I32),
            V(line, F32),
            V(line, F32),
            V((2,) + line, I32),
            V((4,) + bus, F32),
            V((8,) + line, F32),
            V((6,) + line, F32),
            V((240, 256), F32),
            V((2,) + bus, F32),
            V(bus, F32),
            V(line, F32),
            V((1, LANES), F32),
            V((ranks, 1, LANES), F32),
            V((1, LANES), F32),
            V((planes, 1, LANES), F32),
            sem((8,)),
            sem((n_groups,)),
            sem((n_groups,)),
            sem,
            sem,
            sem,
            sem,
        ],
        compiler_params=pltpu.CompilerParams(collective_id=0, has_side_effects=True),
        name="residuals",
    )(consts, delta_state, multipliers, net_inj, ang_grad, status, slack, zdual)
    return mismatch, dual_res, limit_res, norms, total[0, :4]


def solution(mesh):
    placed = (
        P(("ctg", "br")),
        P(("ctg", "br")),
        P("ctg", None, "br"),
        P("ctg", None, "br"),
        P("ctg", None, "br"),
        P("ctg", "br"),
        P("br"),
        P("br"),
        P("ctg", "br"),
        P("br"),
        P("br"),
        P("br"),
        P("br"),
        P("ctg", "br"),
        P("ctg", "br"),
    )
    return jax.shard_map(
        per_device,
        mesh=mesh,
        in_specs=placed,
        out_specs=(P("ctg", None, "br"), P("ctg", "br"), P("ctg", "br"), P("ctg", None), P()),
        check_vma=False,
    )
```

time: 283 us -> 60.4 us (0.21)
  matrix products: 94.7 us -> 0 us
  blocking collectives: 92.8 us -> 0 us
  Pallas kernels: 0 us -> 49 us
  waiting for transfers between devices: 24.1 us -> 0 us
  loops' own time: 20.3 us -> 0 us
  local copies, waits for them, and re-layouts: 24.9 us -> 10.3 us
  between operations: 14.4 us -> 0.7 us
  other arithmetic: 5.73 us -> 0.01 us
  starting transfers between devices: 4.05 us -> 0 us
    dot_general x30 -> x0, matrix products: 94.7 us -> none  [the longest x20 47.9 us: add_block(): jnp.dot(segment, onehot, precision=lax.Precision.HIGHEST, preferred_eleme...]
    all_gather x1 -> x0, blocking collectives: 67.2 us -> none  [turned_gather(): whole = lax.all_gather(both, axis, axis=0, tiled=True)]
    pallas_call x0 -> x1, Pallas kernels: none -> 49 us  [per_device(): pl.pallas_call(functools.partial(kernel, planes, ranks), out_shape=(jax.S...]
    all_to_all x2 -> x0, blocking collectives: 25.6 us -> none  [sent_to_all(): return lax.all_to_all(copies, axis, split_axis=0, concat_axis=0, tiled=True)]
    all_to_all x1 -> x0, waiting for transfers between devices: 24 us -> none  [summed_on_arrival(): lax.all_to_all(in_blocks(array, dim, peers), axis, 0, 0, tiled=True)]
    another operation x3 -> x0, loops' own time: 20.3 us -> none  [the longest x2 13.7 us: select_cols(): result, _ = lax.scan(add_block, start_zero, (tiles, numbers))]
    dynamic_slice x30 -> x0, local copies, waits for them, and re-layouts: 17.6 us -> none  [select_cols(): result, _ = lax.scan(add_block, start_zero, (tiles, numbers))]
    unnamed x25 -> x26, local copies, waits for them, and re-layouts: 2.03 us -> 8.28 us
  transfers between devices with their start and end apart: 2 -> 0, of which waited for: 1 -> 0; matrix products, arithmetic and copies ran while one was open for 1% -> 0% of each run, Pallas kernels for 0% -> 0%
where the time goes in v1:
time: 60.4 us; the launch traced here: 59.9 us
  Pallas kernels  49 us (81%)
  local copies, waits for them, and re-layouts  10.3 us (17%)
  between operations  0.7 us (1%)
    pallas_call x1, Pallas kernels, per_device(): pl.pallas_call(functools.partial(kernel, planes, ranks), out_shape=(jax.S...  49 us
    unnamed x26, local copies, waits for them, and re-layouts  8.28 us
    another operation x9, local copies, waits for them, and re-layouts, per_device(): jnp.stack([from_bus.astype(F32), to_bus.astype(F32), conduct, suscept, ch...  1.46 us

profile of v1, /device:TPU:1, one launch (start us, length us, event | category | flops | bytes accessed | tf_op | source)
XLA Modules:
  0.0 59.9 jit_solution(18395187082037076789)
XLA Ops:
  0.6 0.0 copy-start.2
  0.6 0.7 %stack.29 = f32[1,1664]{1,0:T(1,128)S(1)} reshape(f32[1664]{0:T(1024)} %param.24) | data formatting | bytes 13312 | tf_op jit(solution)/shard_map/stack | solution.py:375
  1.4 0.0 copy-done.2
  1.4 0.0 copy-start.3
  1.4 0.7 %copy-done.3 = f32[1664]{0:T(1024)S(1)} copy-done((f32[1664]{0:T(1024)S(1)}, f32[1664]{0:T(1024)}, u32[]{:S(2)}) %copy-start.3) | copy-done | bytes 6680
  2.1 0.0 copy-start.4
  2.1 0.7 %copy-done.4 = f32[1664]{0:T(1024)S(1)} copy-done((f32[1664]{0:T(1024)S(1)}, f32[1664]{0:T(1024)}, u32[]{:S(2)}) %copy-start.4) | copy-done | bytes 6680
  2.7 0.0 copy-start.8
  2.8 0.6 %copy-done.8 = f32[40]{0:T(128)S(1)} copy-done((f32[40]{0:T(128)S(1)}, f32[40]{0:T(128)}, u32[]{:S(2)}) %copy-start.8) | copy-done | bytes 184
  3.4 0.0 copy-start.9
  3.4 0.6 %copy-done.9 = f32[40]{0:T(128)S(1)} copy-done((f32[40]{0:T(128)S(1)}, f32[40]{0:T(128)}, u32[]{:S(2)}) %copy-start.9) | copy-done | bytes 184
  4.1 0.0 copy-start.5
  4.1 0.7 %copy-done.5 = s32[1664]{0:T(1024)S(1)} copy-done((s32[1664]{0:T(1024)S(1)}, s32[1664]{0:T(1024)}, u32[]{:S(2)}) %copy-start.5) | copy-done | bytes 6680
  4.8 0.0 copy-start.6
  4.8 0.7 %copy-done.6 = s32[1664]{0:T(1024)S(1)} copy-done((s32[1664]{0:T(1024)S(1)}, s32[1664]{0:T(1024)}, u32[]{:S(2)}) %copy-start.6) | copy-done | bytes 6680
  5.5 0.7 %stack.35.consts = f32[8,1664]{1,0:T(8,128)} concatenate(f32[1,1664]{1,0:T(1,128)S(1)} %stack.27, f32[1,1664]{1,0:T(1,128)S(1)} %stack.28, f32[1,1664]{1,0:T(1,128)S(1)} %stack.29, f32[1,1664]{1,0:T(1,128)S(1)} %stack.30, f32[1,1664]{1,0:T(1,128)S(1)} %stack.31, f32[1,1664]{1,0:T(1,128)S(1)} %stack.32, f32[1,1664]{1,0:T(1,128)S(1)} %stack.33, f32[1,1664]{1,0:T(1,128)S(1)} %stack.34), dimensions={0} | concatenate | bytes 106496 | tf_op jit(solution)/shard_map/stack | solution.py:375
  6.2 49.0 %residuals.1 = (f32[8,2,1280]{2,1,0:T(2,128)}, f32[8,1280]{1,0:T(8,128)}, f32[8,1664]{1,0:T(8,128)}, f32[8,4]{1,0:T(8,128)}, f32[1,128]{1,0:T(1,128)}) custom-call(f32[8,1664]{1,0:T(8,128)} %stack.35.consts, f32[8,2,1280]{2,1,0:T(2,128)} %delta.1, f32[8,2,1280]{2,1,0:T(2,128)} %mult.1, f32[8,2,1280]{2,1,0:T(2,128)} %net.1, f32[8,1280]{1,0:T(8,128)} %ang.1, ...), custom_call_target="tpu_custom_call" | custom-call | tf_op jit(solution)/shard_map/residuals/pallas_call | solution.py:393
  55.2 0.0 copy-start.7
  55.2 0.0 copy-start.10
  55.2 0.6 copy-done.10
  55.8 0.5 slice_bitcast_fusion
  56.3 0.0 copy-done.7
  56.3 0.7 %copy.20 = f32[8,4]{0,1:T(4,128)} copy(f32[8,4]{1,0:T(8,128)S(1)} %copy-done.7) | data formatting | bytes 256
  57.0 0.0 copy-start.1
  57.0 1.5 %copy.24 = f32[8,2,1280]{2,1,0:T(2,128)} copy(f32[8,2,1280]{2,1,0:T(2,128)} %get-tuple-element.25) | data formatting | bytes 163840
  58.5 0.0 copy-done.1
  58.5 0.0 copy-start
  58.5 0.6 %copy.25 = f32[8,1280]{1,0:T(8,128)} copy(f32[8,1280]{1,0:T(8,128)S(1)} %copy-done.1) | data formatting | bytes 81920
  59.1 0.2 copy-done
  59.3 0.6 %copy.26 = f32[8,1664]{1,0:T(8,128)} copy(f32[8,1664]{1,0:T(8,128)S(1)} %copy-done) | data formatting | bytes 106496
  (11 shorter events, 0.1 us)
Async XLA Ops:
  0.6 0.7 %copy-start.2 = (f32[1664]{0:T(1024)S(1)}, f32[1664]{0:T(1024)}, u32[]{:S(2)}) copy-start(f32[1664]{0:T(1024)} %param.25) | copy-start | bytes 19972
  1.4 0.7 %copy-start.3 = (f32[1664]{0:T(1024)S(1)}, f32[1664]{0:T(1024)}, u32[]{:S(2)}) copy-start(f32[1664]{0:T(1024)} %param.26) | copy-start | bytes 19972
  2.1 0.7 %copy-start.4 = (f32[1664]{0:T(1024)S(1)}, f32[1664]{0:T(1024)}, u32[]{:S(2)}) copy-start(f32[1664]{0:T(1024)} %param.27) | copy-start | bytes 19972
  2.7 0.7 %copy-start.8 = (f32[40]{0:T(128)S(1)}, f32[40]{0:T(128)}, u32[]{:S(2)}) copy-start(f32[40]{0:T(128)} %param.15) | copy-start | bytes 484
  3.4 0.7 %copy-start.9 = (f32[40]{0:T(128)S(1)}, f32[40]{0:T(128)}, u32[]{:S(2)}) copy-start(f32[40]{0:T(128)} %param.16) | copy-start | bytes 484
  4.1 0.7 %copy-start.5 = (s32[1664]{0:T(1024)S(1)}, s32[1664]{0:T(1024)}, u32[]{:S(2)}) copy-start(s32[1664]{0:T(1024)} %param.21) | copy-start | bytes 19972
  4.8 0.7 %copy-start.6 = (s32[1664]{0:T(1024)S(1)}, s32[1664]{0:T(1024)}, u32[]{:S(2)}) copy-start(s32[1664]{0:T(1024)} %param.22) | copy-start | bytes 19972
  55.2 1.1 %copy-start.7 = (f32[8,4]{1,0:T(8,128)S(1)}, f32[8,4]{1,0:T(8,128)}, u32[]{:S(2)}) copy-start(f32[8,4]{1,0:T(8,128)} %get-tuple-element.18) | copy-start | bytes 388
  55.2 0.6 %copy-start.10 = (f32[1,128]{1,0:T(1,128)S(1)}, f32[1,128]{1,0:T(1,128)}, u32[]{:S(2)}) copy-start(f32[1,128]{1,0:T(1,128)} %get-tuple-element.14) | copy-start | bytes 1540
  57.0 1.5 %copy-start.1 = (f32[8,1280]{1,0:T(8,128)S(1)}, f32[8,1280]{1,0:T(8,128)}, u32[]{:S(2)}) copy-start(f32[8,1280]{1,0:T(8,128)} %get-tuple-element.26) | copy-start | bytes 122884
  58.5 0.8 %copy-start = (f32[8,1664]{1,0:T(8,128)S(1)}, f32[8,1664]{1,0:T(8,128)}, u32[]{:S(2)}) copy-start(f32[8,1664]{1,0:T(8,128)} %get-tuple-element.27) | copy-start | bytes 159748

commit v2 on v1

v2 whole, which is shorter than its diff:
```python
import functools

import jax
import jax.numpy as jnp
from jax import lax
from jax.experimental import pallas as pl
from jax.experimental.pallas import tpu as pltpu
from jax.sharding import PartitionSpec as P

F32, I32, BF16 = jnp.float32, jnp.int32, jnp.bfloat16
LANES = 128
MESH = pl.DeviceIdType.MESH


def kernel(
    planes,
    ranks,
    base_vm,
    base_va,
    from_bus,
    to_bus,
    conduct,
    suscept,
    charging,
    rating,
    delta,
    mult,
    net,
    ang,
    status,
    slack,
    zdual,
    mismatch,
    dual,
    limit,
    norms,
    total,
    lines_i,
    lines_f,
    delta_v,
    mult_v,
    net_v,
    ang_v,
    status_v,
    slack_v,
    zdual_v,
    base_v,
    base_z,
    base_all,
    idx,
    coef,
    mult_all,
    delta_all,
    net_all,
    ang_all,
    status_all,
    slack_all,
    tables,
    ends,
    terms,
    sums,
    mis_out,
    dual_out,
    limit_out,
    sq_mine,
    sq_all,
    tot_mine,
    tot_all,
    load_sem,
    send_sem,
    recv_sem,
    pass_send,
    pass_recv,
    base_send,
    base_recv,
    tot_send,
    tot_recv,
):
    me = lax.axis_index("ctg")
    rank = lax.axis_index("br")
    core = lax.rem(me, 2)
    partner = me + 1 - 2 * core
    nbus = delta.shape[2]
    nline = status.shape[1]
    bus_tiles, line_tiles = nbus // LANES, nline // LANES

    pairs = (
        (from_bus, lines_i.at[0]),
        (to_bus, lines_i.at[1]),
        (mult, mult_v),
        (delta, delta_v),
        (conduct, lines_f.at[0]),
        (suscept, lines_f.at[1]),
        (charging, lines_f.at[2]),
        (rating, lines_f.at[3]),
        (status, status_v),
        (slack, slack_v),
        (net, net_v),
        (ang, ang_v),
        (zdual, zdual_v),
    )
    loads = [pltpu.make_async_copy(a, b, load_sem.at[n]) for n, (a, b) in enumerate(pairs)]
    for c in loads:
        c.start()

    barrier = pltpu.get_barrier_semaphore()
    for d in range(1, ranks):
        pl.semaphore_signal(barrier, 1, device_id=(me, lax.rem(rank + d, ranks)), device_id_type=MESH)

    def greet(d, carry):
        pl.semaphore_signal(barrier, 1, device_id=(lax.rem(me + d, planes), rank), device_id_type=MESH)
        return carry

    lax.fori_loop(1, planes, greet, 0)
    piece = base_vm.shape[1]
    base_v[0:1, 0:piece] = base_vm[...]
    base_v[1:2, 0:piece] = base_va[...]
    for c in loads:
        c.wait()

    lane8 = lax.broadcasted_iota(I32, (ranks, LANES), 1)
    row8 = lax.broadcasted_iota(I32, (ranks, LANES), 0)
    comp_sq = jnp.zeros((ranks, LANES), F32)
    for t in range(line_tiles):
        cols = slice(t * LANES, (t + 1) * LANES)
        comp = status_v[:, cols].astype(F32) * (zdual_v[:, cols] * slack_v[:, cols] - 0.01)
        comp_sq += comp * comp
    comp_sum = jnp.sum(comp_sq, axis=1, keepdims=True)
    comp_row = jnp.sum(jnp.where(lane8 == row8 + 8, comp_sum, 0.0), axis=0, keepdims=True)

    pl.semaphore_wait(barrier, ranks - 1 + planes - 1)

    half = lambda ref: ref.at[pl.ds(2 * core, 2)]
    groups = (
        (lambda s: base_v, lambda r: base_z.at[r], base_z),
        (lambda s: lines_i.at[core], lambda r: idx.at[core, :, r, :], idx.at[core]),
        (lambda s: mult_v.at[s], lambda r: mult_all.at[:, r, :], mult_all),
        (lambda s: delta_v.at[s], lambda r: delta_all.at[:, r, :], delta_all),
        (lambda s: half(lines_f), lambda r: coef.at[pl.ds(2 * core, 2), :, r, :], half(coef)),
        (lambda s: status_v.at[s], lambda r: status_all.at[r], status_all),
        (lambda s: slack_v.at[s], lambda r: slack_all.at[r], slack_all),
        (lambda s: net_v.at[s], lambda r: net_all.at[:, r, :], net_all),
        (lambda s: ang_v.at[s], lambda r: ang_all.at[r], ang_all),
    )

    def send(n, source, place):
        pltpu.make_async_copy(source(rank), place(rank), recv_sem.at[n]).start()
        for d in range(1, ranks):
            peer = lax.rem(rank + d, ranks)
            pltpu.make_async_remote_copy(
                src_ref=source(peer),
                dst_ref=place(rank),
                send_sem=send_sem.at[n],
                recv_sem=recv_sem.at[n],
                device_id=(me, peer),
                device_id_type=MESH,
            ).start()

    def take(n, whole):
        pltpu.make_async_copy(whole, whole, recv_sem.at[n]).wait()

    for n, (source, place, _) in enumerate(groups):
        send(n, source, place)

    def across(n, mine, theirs):
        out = pltpu.make_async_remote_copy(
            src_ref=mine,
            dst_ref=mine,
            send_sem=pass_send.at[n],
            recv_sem=pass_recv.at[n],
            device_id=(partner, rank),
            device_id_type=MESH,
        )
        out.start()
        return out, pltpu.make_async_copy(theirs, theirs, pass_recv.at[n])

    take(0, base_z)
    group = planes // ranks
    home = base_all.at[lax.rem(me, group), :, :, me // group, :]
    pltpu.make_async_copy(base_z, home, base_recv).start()

    def spread(d, carry):
        pltpu.make_async_remote_copy(
            src_ref=base_z,
            dst_ref=home,
            send_sem=base_send,
            recv_sem=base_recv,
            device_id=(lax.rem(me + d, planes), rank),
            device_id_type=MESH,
        ).start()
        return carry

    lax.fori_loop(1, planes, spread, 0)

    take(1, idx.at[core])
    idx_out, idx_in = across(0, idx.at[core], idx.at[1 - core])
    take(2, mult_all)
    idx_in.wait()

    def look_up(first, k):
        for e in range(2):
            where_to = idx[e, k]
            high, low = where_to >> 7, where_to & 127
            found = [jnp.zeros((ranks, LANES), F32) for _ in range(2)]
            for h in range(ranks * bus_tiles):
                here = high == h
                r, t = h // bus_tiles, h % bus_tiles
                for q in range(2):
                    src = mult_all if first else tables
                    row = jnp.broadcast_to(src[q, r : r + 1, t * LANES : (t + 1) * LANES], (ranks, LANES))
                    got = jnp.take_along_axis(row, low, axis=1, mode="promise_in_bounds")
                    found[q] = jnp.where(here, got, found[q])
            for q in range(2):
                ends[4 * e + 2 * first + q, k] = found[q]

    def gather_mult(k, carry):
        look_up(1, k)
        return carry

    lax.fori_loop(0, line_tiles, gather_mult, 0)

    take(3, delta_all)
    pltpu.make_async_copy(base_all, base_all, base_recv).wait()
    for q in range(2):
        tiles = [jnp.zeros((ranks, LANES), F32) for _ in range(bus_tiles)]
        for p in range(nbus // piece):
            rows = base_all[p // ranks, p % ranks, q]
            t, off = p * piece // LANES, p * piece % LANES
            moved = pltpu.roll(rows, off, 1) if off else rows
            tiles[t] = jnp.where((lane8 >= off) & (lane8 < off + piece), moved, tiles[t])
            if off + piece > LANES:
                tiles[t + 1] = jnp.where(lane8 < off + piece - LANES, moved, tiles[t + 1])
        for t in range(bus_tiles):
            cols = slice(t * LANES, (t + 1) * LANES)
            tables[q, :, cols] = tiles[t] + delta_all[q, :, cols]

    take(4, half(coef))
    coef_out, coef_in = across(1, half(coef), coef.at[pl.ds(2 - 2 * core, 2)])

    def gather_volt(k, carry):
        look_up(0, k)
        return carry

    lax.fori_loop(0, line_tiles, gather_volt, 0)

    coef_in.wait()
    take(5, status_all)

    def flows(k, carry):
        cols = pl.ds(pl.multiple_of(k * LANES, LANES), LANES)
        vf, af, mpf, mqf = (ends[q, k] for q in range(4))
        vt, at, mpt, mqt = (ends[4 + q, k] for q in range(4))
        g, b, h = (coef[q, k] for q in range(3))
        live = status_all[:, cols].astype(F32)
        diff = af - at
        cs, sn = jnp.cos(diff), jnp.sin(diff)
        u = vf * vt
        gcs, gsn, bcs, bsn = g * cs, g * sn, b * cs, b * sn
        pf = (g * vf * vf - u * (gcs + bsn)) * live
        qf = (-(b + h) * vf * vf - u * (gsn - bcs)) * live
        pt = (g * vt * vt - u * (gcs - bsn)) * live
        qt = (-(b + h) * vt * vt + u * (gsn + bcs)) * live
        fd = u * (mpf * (gsn - bcs) - mqf * (gcs + bsn) + mpt * (gsn + bcs) + mqt * (gcs - bsn)) * live
        for n, v in enumerate((pf, qf, fd, pt, qt, -fd)):
            terms[n, k] = v
        return carry

    lax.fori_loop(0, line_tiles, flows, 0)

    take(6, slack_all)
    limit_sq = jnp.zeros((ranks, LANES), F32)
    for k in range(line_tiles):
        cols = slice(k * LANES, (k + 1) * LANES)
        pf, qf = terms[0, k], terms[1, k]
        live = status_all[:, cols].astype(F32)
        lim = live * (pf * pf + qf * qf + slack_all[:, cols] - coef[3, k] * coef[3, k])
        limit_out[:, cols] = lim
        limit_sq += lim * lim

    n_limit, n_mis, n_dual, n_sq = (len(groups) + n for n in range(4))
    send(n_limit, lambda s: limit_out.at[s], lambda r: limit.at[r])

    row16 = lax.broadcasted_iota(I32, (16, LANES), 0)
    per = nbus // 256
    high_of = [((row16 & 7) * per + j).astype(F32).astype(BF16) for j in range(per)]
    low_of = row16.astype(F32).astype(BF16)
    none16, one16 = jnp.zeros((16, LANES), BF16), jnp.ones((16, LANES), BF16)
    sums[...] = jnp.zeros_like(sums)

    def scatter(k, carry):
        for s in range(ranks):
            left, right = [], []
            for e in range(2):
                at_bus = idx[e, k, s : s + 1, :]
                high = jnp.broadcast_to((at_bus >> 8).astype(F32), (16, LANES)).astype(BF16)
                low = jnp.broadcast_to((at_bus & 255).astype(F32), (16, LANES)).astype(BF16)
                vals = []
                for r in range(3):
                    v = terms[3 * e + r, k, s : s + 1, :]
                    coarse = v.astype(BF16).astype(F32)
                    fine = v - coarse
                    vals.append(
                        jnp.concatenate(
                            [jnp.broadcast_to(coarse, (8, LANES)), jnp.broadcast_to(fine, (8, LANES))], 0
                        ).astype(BF16)
                    )
                rows = []
                for j in range(per):
                    here = high == high_of[j]
                    rows += [jnp.where(here, v, none16) for v in vals]
                left.append(jnp.concatenate(rows, 0))
                right.append(
                    jnp.concatenate(
                        [jnp.where(low == low_of + BF16(16 * t), one16, none16) for t in range(16)], 0
                    )
                )
            sums[...] += lax.dot_general(
                jnp.concatenate(left, 1),
                jnp.concatenate(right, 1),
                (((1,), (1,)), ((), ())),
                preferred_element_type=F32,
            )
        return carry

    lax.fori_loop(0, line_tiles, scatter, 0)

    take(7, net_all)
    take(8, ang_all)
    mis_sq, dual_sq = jnp.zeros((ranks, 256), F32), jnp.zeros((ranks, 256), F32)
    for j in range(per):
        cols = slice(256 * j, 256 * (j + 1))
        for r in range(3):
            first = (3 * j + r) * 16
            got = sums[first : first + 8, :] + sums[first + 8 : first + 16, :]
            if r < 2:
                out = got - net_all[r, :, cols]
                mis_out[r, :, cols] = out
                mis_sq += out * out
            else:
                out = got + ang_all[:, cols]
                dual_out[:, cols] = out
                dual_sq += out * out

    mine = comp_row
    for n, part in enumerate((mis_sq, dual_sq, limit_sq)):
        mine = jnp.where(lane8[0:1] == n, jnp.sum(part, keepdims=True), mine)
    sq_mine[...] = mine
    send(n_sq, lambda s: sq_mine, lambda r: sq_all.at[r])
    send(n_mis, lambda s: mis_out.at[:, s, :], lambda r: mismatch.at[r])
    send(n_dual, lambda s: dual_out.at[s], lambda r: dual.at[r])

    take(n_sq, sq_all)
    every = sq_all[:, 0, :]
    comp_all = jnp.sum(every, axis=0, keepdims=True)
    comp_of = jnp.sum(jnp.where(lane8 == row8 + 8, comp_all, 0.0), axis=1, keepdims=True)
    squares = jnp.where(lane8 == 3, comp_of, jnp.where(lane8 < 3, every, 0.0))
    tot_mine[...] = jnp.sum(squares, axis=0, keepdims=True)
    pltpu.make_async_copy(tot_mine, tot_all.at[me], tot_recv).start()

    def share(d, carry):
        pltpu.make_async_remote_copy(
            src_ref=tot_mine,
            dst_ref=tot_all.at[me],
            send_sem=tot_send,
            recv_sem=tot_recv,
            device_id=(lax.rem(me + d, planes), rank),
            device_id_type=MESH,
        ).start()
        return carry

    lax.fori_loop(1, planes, share, 0)
    norms[...] = jnp.sqrt(squares)
    take(n_limit, limit)
    take(n_mis, mismatch)
    take(n_dual, dual)
    idx_out.wait_send()
    coef_out.wait_send()
    for n, (_, _, dest) in enumerate(groups):
        sent(send_sem.at[n], dest, ranks)
    for n, dest in ((n_limit, limit), (n_mis, mismatch), (n_dual, dual), (n_sq, sq_all)):
        sent(send_sem.at[n], dest, ranks)
    part = base_all.at[:, :, :, 0 : ranks - 1, :]
    pltpu.make_async_copy(part, part, base_send).wait()
    part = base_all.at[0 : group - 1, :, :, ranks - 1, :]
    pltpu.make_async_copy(part, part, base_send).wait()
    pltpu.make_async_copy(tot_all, tot_all, tot_recv).wait()
    whole = jnp.sum(tot_all[:, 0, :], axis=0, keepdims=True)
    total[...] = jnp.sqrt(whole / (planes * ranks))
    part = tot_all.at[0 : planes - 1]
    pltpu.make_async_copy(part, part, tot_send).wait()


def sent(sem, dest, ranks):
    dim = len(dest.shape) - 1 - dest.shape[::-1].index(ranks)
    part = dest.at[(slice(None),) * dim + (slice(0, ranks - 1),)]
    pltpu.make_async_copy(part, part, sem).wait()


def hand_out(norms, total, mis, dual, limit, norms_out, total_out, mis_out, dual_out, limit_out, sem):
    pairs = ((mis, mis_out), (dual, dual_out), (limit, limit_out))
    copies = [pltpu.make_async_copy(a, b, sem.at[n]) for n, (a, b) in enumerate(pairs)]
    for c in copies:
        c.start()
    norms_out[...] = norms[...].T[0:4, :]
    total_out[...] = total[:, 0:4]
    for c in copies:
        c.wait()


def per_device(
    base_vm,
    base_va,
    delta_state,
    multipliers,
    net_inj,
    ang_grad,
    from_bus,
    to_bus,
    status,
    conduct,
    suscept,
    charging,
    rating,
    slack,
    zdual,
):
    planes, ranks = lax.axis_size("ctg"), lax.axis_size("br")
    nscen, _, nbus = delta_state.shape
    nline = status.shape[1]
    tiles = nline // LANES
    hbm = pl.BlockSpec(memory_space=pl.ANY)
    vmem = pl.BlockSpec(memory_space=pltpu.VMEM)
    V = pltpu.VMEM
    bus, line, deep = (ranks, nbus), (ranks, nline), (tiles, ranks, LANES)
    sem = pltpu.SemaphoreType.DMA
    row = lambda a: a.reshape(1, -1)
    grid = lambda a: a.reshape(tiles, LANES)
    results = pl.pallas_call(
        functools.partial(kernel, planes, ranks),
        out_shape=(
            V((nscen, 2, nbus), F32),
            V((nscen, nbus), F32),
            V((nscen, nline), F32),
            V((nscen, LANES), F32),
            V((1, LANES), F32),
        ),
        in_specs=[vmem] * 2 + [hbm] * 13,
        out_specs=(vmem,) * 5,
        scratch_shapes=[
            V((2, tiles, LANES), I32),
            V((4, tiles, LANES), F32),
            V((nscen, 2, nbus), F32),
            V((nscen, 2, nbus), F32),
            V((nscen, 2, nbus), F32),
            V((nscen, nbus), F32),
            V((nscen, nline), I32),
            V((nscen, nline), F32),
            V((nscen, nline), F32),
            V((2, LANES), F32),
            V((ranks, 2, LANES), F32),
            V((planes // ranks, ranks, 2, ranks, LANES), F32),
            V((2,) + deep, I32),
            V((4,) + deep, F32),
            V((2,) + bus, F32),
            V((2,) + bus, F32),
            V((2,) + bus, F32),
            V(bus, F32),
            V(line, I32),
            V(line, F32),
            V((2,) + bus, F32),
            V((8,) + deep, F32),
            V((6,) + deep, F32),
            V((240, 256), F32),
            V((2,) + bus, F32),
            V(bus, F32),
            V(line, F32),
            V((1, LANES), F32),
            V((ranks, 1, LANES), F32),
            V((1, LANES), F32),
            V((planes, 1, LANES), F32),
            sem((13,)),
            sem((13,)),
            sem((13,)),
            sem((2,)),
            sem((2,)),
            sem,
            sem,
            sem,
            sem,
        ],
        compiler_params=pltpu.CompilerParams(collective_id=0, has_side_effects=True),
        name="residuals",
    )(
        row(base_vm),
        row(base_va),
        grid(from_bus),
        grid(to_bus),
        grid(conduct),
        grid(suscept),
        grid(charging),
        grid(rating),
        delta_state,
        multipliers,
        net_inj,
        ang_grad,
        status,
        slack,
        zdual,
    )
    mis, dual, limit, norms, total = (pltpu.with_memory_space_constraint(r, V) for r in results)
    norms, total, mis, dual, limit = pl.pallas_call(
        hand_out,
        out_shape=(
            jax.ShapeDtypeStruct((4, nscen), F32),
            jax.ShapeDtypeStruct((1, 4), F32),
            jax.ShapeDtypeStruct((nscen, 2, nbus), F32),
            jax.ShapeDtypeStruct((nscen, nbus), F32),
            jax.ShapeDtypeStruct((nscen, nline), F32),
        ),
        in_specs=[vmem] * 5,
        out_specs=(vmem, vmem, hbm, hbm, hbm),
        scratch_shapes=[sem((3,))],
        name="hand_out",
    )(norms, total, mis, dual, limit)
    return mis, dual, limit, norms.T, total.reshape(4)


def solution(mesh):
    placed = (
        P(("ctg", "br")),
        P(("ctg", "br")),
        P("ctg", None, "br"),
        P("ctg", None, "br"),
        P("ctg", None, "br"),
        P("ctg", "br"),
        P("br"),
        P("br"),
        P("ctg", "br"),
        P("br"),
        P("br"),
        P("br"),
        P("br"),
        P("ctg", "br"),
        P("ctg", "br"),
    )
    return jax.shard_map(
        per_device,
        mesh=mesh,
        in_specs=placed,
        out_specs=(P("ctg", None, "br"), P("ctg", "br"), P("ctg", "br"), P("ctg", None), P()),
        check_vma=False,
    )
```

time: 60.4 us -> 48.9 us (0.81)
  local copies, waits for them, and re-layouts: 10.3 us -> 0 us
  Pallas kernels: 49 us -> 48.1 us
    unnamed x26 -> x0, local copies, waits for them, and re-layouts: 8.28 us -> none
    another operation x9 -> x0, local copies, waits for them, and re-layouts: 1.46 us -> none  [per_device(): jnp.stack([from_bus.astype(F32), to_bus.astype(F32), conduct, suscept, ch...]
    pallas_call x1 -> x2, Pallas kernels: 49 us -> 48.1 us  [the longest x1 46.8 us: per_device(): pl.pallas_call(functools.partial(kernel, planes, ranks), out_shape=(V((ns...]
where the time goes in v2:
time: 48.9 us; the launch traced here: 48.8 us
  Pallas kernels  48.1 us (98%)
  between operations  0.65 us (1%)
    pallas_call x1, Pallas kernels, per_device(): pl.pallas_call(functools.partial(kernel, planes, ranks), out_shape=(V((ns...  46.8 us
    pallas_call x1, Pallas kernels, per_device(): pl.pallas_call(hand_out, out_shape=(jax.ShapeDtypeStruct((4, nscen), F32)...  1.27 us

profile of v2, /device:TPU:1, one launch (start us, length us, event | category | flops | bytes accessed | tf_op | source)
XLA Modules:
  0.0 48.8 jit_solution(12894514099352592789)
XLA Ops:
  0.6 46.8 %residuals.1 = (f32[8,2,1280]{2,1,0:T(2,128)S(1)}, f32[8,1280]{1,0:T(8,128)S(1)}, f32[8,1664]{1,0:T(8,128)S(1)}, f32[8,128]{1,0:T(8,128)S(1)}, f32[1,128]{1,0:T(1,128)S(1)}) custom-call(f32[1,40]{1,0:T(1,128)} %bitcast.16, f32[1,40]{1,0:T(1,128)} %bitcast.17, s32[13,128]{1,0:T(8,128)} %bitcast.10, s32[13,128]{1,0:T(8,128)} %bitcast.11, f32[13,128]{1,0:T(8,128)} %bitcast.12, ...), custom_call_target="tpu_custom_call" | custom-call | tf_op jit(solution)/shard_map/residuals/pallas_call | solution.py:438
  47.5 1.3 %hand_out.1 = (f32[4,8]{1,0:T(4,128)}, f32[1,4]{1,0:T(1,128)}, f32[8,2,1280]{2,1,0:T(2,128)}, f32[8,1280]{1,0:T(8,128)}, f32[8,1664]{1,0:T(8,128)}) custom-call(f32[8,128]{1,0:T(8,128)S(1)} %get-tuple-element.15.norms, f32[1,128]{1,0:T(1,128)S(1)} %get-tuple-element.16.total, f32[8,2,1280]{2,1,0:T(2,128)S(1)} %get-tuple-element.17.mis, ...), custom_call_target="tpu_custom_call" | custom-call | tf_op jit(solution)/shard_map/hand_out/pallas_call | solution.py:511

commit v3 on v2

--- a/solution.py
+++ b/solution.py
@@ -55,7 +55,8 @@
     ang_all,
     status_all,
     slack_all,
-    tables,
+    angles,
+    stacked,
     ends,
     terms,
     sums,
@@ -197,24 +198,74 @@
     take(2, mult_all)
     idx_in.wait()
 
-    def look_up(first, k):
+    row16 = lax.broadcasted_iota(I32, (16, LANES), 0)
+    ramp16 = row16.astype(F32).astype(BF16)
+    none16, one16 = jnp.zeros((16, LANES), BF16), jnp.ones((16, LANES), BF16)
+    high_row = [row8 * bus_tiles + t for t in range(bus_tiles)]
+    n_rows = ranks * bus_tiles
+
+    def one_hot(low, tiles):
+        low = jnp.broadcast_to(low.astype(F32), (16, LANES)).astype(BF16)
+        return jnp.concatenate(
+            [jnp.where(low == ramp16 + BF16(16 * t), one16, none16) for t in range(tiles)], 0
+        )
+
+    def stack(q, tile):
+        for t in range(0, bus_tiles, 2):
+            both = jnp.concatenate([tile(t), tile(t + 1)], 0)
+            coarse = both.astype(BF16)
+            rows = slice(q * n_rows + ranks * t, q * n_rows + ranks * (t + 2))
+            stacked[rows, 0:LANES] = coarse
+            stacked[rows, LANES:] = (both - coarse.astype(F32)).astype(BF16)
+
+    def by_matmul(k, count, store):
         for e in range(2):
-            where_to = idx[e, k]
-            high, low = where_to >> 7, where_to & 127
-            found = [jnp.zeros((ranks, LANES), F32) for _ in range(2)]
-            for h in range(ranks * bus_tiles):
-                here = high == h
+            out = [jnp.zeros((ranks, LANES), F32) for _ in range(count)]
+            for s in range(0, ranks, 2):
+                hot, high = [], []
+                for n in range(2):
+                    bus = idx[e, k, s + n : s + n + 1, :]
+                    high.append(jnp.broadcast_to(bus >> 7, (ranks, LANES)))
+                    hot.append(one_hot(bus & 127, LANES // 16))
+                hot = jnp.concatenate(hot, 1)
+                rows = jnp.dot(
+                    stacked[0 : count * n_rows, :],
+                    jnp.concatenate([hot, hot], 0),
+                    preferred_element_type=F32,
+                )
+                for n in range(2):
+                    for q in range(count):
+                        acc = jnp.zeros((ranks, LANES), F32)
+                        for t in range(bus_tiles):
+                            first = q * n_rows + ranks * t
+                            part = rows[first : first + ranks, n * LANES : (n + 1) * LANES]
+                            acc = jnp.where(high[n] == high_row[t], part, acc)
+                        for step in (4, 2, 1):
+                            acc = acc + pltpu.roll(acc, step, 0)
+                        out[q] = jnp.where(row8 == s + n, acc, out[q])
+            for q in range(count):
+                store(e, q, out[q])
+
+    def by_permute(k, store):
+        for e in range(2):
+            bus = idx[e, k]
+            high, low = bus >> 7, bus & 127
+            found = jnp.zeros((ranks, LANES), F32)
+            for h in range(n_rows):
                 r, t = h // bus_tiles, h % bus_tiles
-                for q in range(2):
-                    src = mult_all if first else tables
-                    row = jnp.broadcast_to(src[q, r : r + 1, t * LANES : (t + 1) * LANES], (ranks, LANES))
-                    got = jnp.take_along_axis(row, low, axis=1, mode="promise_in_bounds")
-                    found[q] = jnp.where(here, got, found[q])
-            for q in range(2):
-                ends[4 * e + 2 * first + q, k] = found[q]
+                row = jnp.broadcast_to(angles[r : r + 1, t * LANES : (t + 1) * LANES], (ranks, LANES))
+                got = jnp.take_along_axis(row, low, axis=1, mode="promise_in_bounds")
+                found = jnp.where(high == h, got, found)
+            store(e, found)
+
+    for q in range(2):
+        stack(q, lambda t: mult_all[q, :, t * LANES : (t + 1) * LANES])
 
     def gather_mult(k, carry):
-        look_up(1, k)
+        def store(e, q, value):
+            ends[4 * e + 2 + q, k] = value
+
+        by_matmul(k, 2, store)
         return carry
 
     lax.fori_loop(0, line_tiles, gather_mult, 0)
@@ -232,13 +283,24 @@
                 tiles[t + 1] = jnp.where(lane8 < off + piece - LANES, moved, tiles[t + 1])
         for t in range(bus_tiles):
             cols = slice(t * LANES, (t + 1) * LANES)
-            tables[q, :, cols] = tiles[t] + delta_all[q, :, cols]
+            tiles[t] = tiles[t] + delta_all[q, :, cols]
+            if q == 1:
+                angles[:, cols] = tiles[t]
+        if q == 0:
+            stack(0, lambda t: tiles[t] - 1.0)
 
     take(4, half(coef))
     coef_out, coef_in = across(1, half(coef), coef.at[pl.ds(2 - 2 * core, 2)])
 
     def gather_volt(k, carry):
-        look_up(0, k)
+        def store_vm(e, q, value):
+            ends[4 * e, k] = value + 1.0
+
+        def store_va(e, value):
+            ends[4 * e + 1, k] = value
+
+        by_permute(k, store_va)
+        by_matmul(k, 1, store_vm)
         return carry
 
     lax.fori_loop(0, line_tiles, gather_volt, 0)
@@ -280,11 +342,8 @@
     n_limit, n_mis, n_dual, n_sq = (len(groups) + n for n in range(4))
     send(n_limit, lambda s: limit_out.at[s], lambda r: limit.at[r])
 
-    row16 = lax.broadcasted_iota(I32, (16, LANES), 0)
     per = nbus // 256
     high_of = [((row16 & 7) * per + j).astype(F32).astype(BF16) for j in range(per)]
-    low_of = row16.astype(F32).astype(BF16)
-    none16, one16 = jnp.zeros((16, LANES), BF16), jnp.ones((16, LANES), BF16)
     sums[...] = jnp.zeros_like(sums)
 
     def scatter(k, carry):
@@ -293,7 +352,6 @@
             for e in range(2):
                 at_bus = idx[e, k, s : s + 1, :]
                 high = jnp.broadcast_to((at_bus >> 8).astype(F32), (16, LANES)).astype(BF16)
-                low = jnp.broadcast_to((at_bus & 255).astype(F32), (16, LANES)).astype(BF16)
                 vals = []
                 for r in range(3):
                     v = terms[3 * e + r, k, s : s + 1, :]
@@ -309,11 +367,7 @@
                     here = high == high_of[j]
                     rows += [jnp.where(here, v, none16) for v in vals]
                 left.append(jnp.concatenate(rows, 0))
-                right.append(
-                    jnp.concatenate(
-                        [jnp.where(low == low_of + BF16(16 * t), one16, none16) for t in range(16)], 0
-                    )
-                )
+                right.append(one_hot(at_bus & 255, 16))
             sums[...] += lax.dot_general(
                 jnp.concatenate(left, 1),
                 jnp.concatenate(right, 1),
@@ -467,7 +521,8 @@
             V(bus, F32),
             V(line, I32),
             V(line, F32),
-            V((2,) + bus, F32),
+            V(bus, F32),
+            V((2 * nbus // LANES * ranks, 2 * LANES), BF16),
             V((8,) + deep, F32),
             V((6,) + deep, F32),
             V((240, 256), F32),

time: 48.9 us -> 47.1 us (0.963)
  Pallas kernels: 48.1 us -> 46.3 us
    pallas_call x1, Pallas kernels: 46.8 us -> 45 us  [per_device(): pl.pallas_call(functools.partial(kernel, planes, ranks), out_shape=(V((ns...]
where the time goes in v3:
time: 47.1 us; the launch traced here: 46.9 us
  Pallas kernels  46.3 us (98%)
  between operations  0.65 us (1%)
    pallas_call x1, Pallas kernels, per_device(): pl.pallas_call(functools.partial(kernel, planes, ranks), out_shape=(V((ns...  45 us
    pallas_call x1, Pallas kernels, per_device(): pl.pallas_call(hand_out, out_shape=(jax.ShapeDtypeStruct((4, nscen), F32)...  1.27 us

profile of v3, /device:TPU:1, one launch (start us, length us, event | category | flops | bytes accessed | tf_op | source)
XLA Modules:
  0.0 46.9 jit_solution(6414512348000400091)
XLA Ops:
  0.6 45.0 %residuals.1 = (f32[8,2,1280]{2,1,0:T(2,128)S(1)}, f32[8,1280]{1,0:T(8,128)S(1)}, f32[8,1664]{1,0:T(8,128)S(1)}, f32[8,128]{1,0:T(8,128)S(1)}, f32[1,128]{1,0:T(1,128)S(1)}) custom-call(f32[1,40]{1,0:T(1,128)} %bitcast.16, f32[1,40]{1,0:T(1,128)} %bitcast.17, s32[13,128]{1,0:T(8,128)} %bitcast.10, s32[13,128]{1,0:T(8,128)} %bitcast.11, f32[13,128]{1,0:T(8,128)} %bitcast.12, ...), custom_call_target="tpu_custom_call" | custom-call | tf_op jit(solution)/shard_map/residuals/pallas_call | solution.py:492
  45.7 1.3 %hand_out.1 = (f32[4,8]{1,0:T(4,128)}, f32[1,4]{1,0:T(1,128)}, f32[8,2,1280]{2,1,0:T(2,128)}, f32[8,1280]{1,0:T(8,128)}, f32[8,1664]{1,0:T(8,128)}) custom-call(f32[8,128]{1,0:T(8,128)S(1)} %get-tuple-element.15.norms, f32[1,128]{1,0:T(1,128)S(1)} %get-tuple-element.16.total, f32[8,2,1280]{2,1,0:T(2,128)S(1)} %get-tuple-element.17.mis, ...), custom_call_target="tpu_custom_call" | custom-call | tf_op jit(solution)/shard_map/hand_out/pallas_call | solution.py:566

commit v4 on v3

--- a/solution.py
+++ b/solution.py
@@ -268,7 +268,7 @@
         by_matmul(k, 2, store)
         return carry
 
-    lax.fori_loop(0, line_tiles, gather_mult, 0)
+    lax.fori_loop(0, line_tiles, gather_mult, 0, unroll=True)
 
     take(3, delta_all)
     pltpu.make_async_copy(base_all, base_all, base_recv).wait()
@@ -303,7 +303,7 @@
         by_matmul(k, 1, store_vm)
         return carry
 
-    lax.fori_loop(0, line_tiles, gather_volt, 0)
+    lax.fori_loop(0, line_tiles, gather_volt, 0, unroll=True)
 
     coef_in.wait()
     take(5, status_all)
@@ -327,7 +327,7 @@
             terms[n, k] = v
         return carry
 
-    lax.fori_loop(0, line_tiles, flows, 0)
+    lax.fori_loop(0, line_tiles, flows, 0, unroll=True)
 
     take(6, slack_all)
     limit_sq = jnp.zeros((ranks, LANES), F32)
@@ -376,7 +376,7 @@
             )
         return carry
 
-    lax.fori_loop(0, line_tiles, scatter, 0)
+    lax.fori_loop(0, line_tiles, scatter, 0, unroll=True)
 
     take(7, net_all)
     take(8, ang_all)

time: 47.1 us -> 42.1 us (0.89)
  Pallas kernels: 46.3 us -> 41.3 us
    pallas_call x1, Pallas kernels: 45 us -> 40.1 us  [per_device(): pl.pallas_call(functools.partial(kernel, planes, ranks), out_shape=(V((ns...]
where the time goes in v4:
time: 42.1 us; the launch traced here: 42 us
  Pallas kernels  41.3 us (98%)
  between operations  0.65 us (2%)
    pallas_call x1, Pallas kernels, per_device(): pl.pallas_call(functools.partial(kernel, planes, ranks), out_shape=(V((ns...  40.1 us
    pallas_call x1, Pallas kernels, per_device(): pl.pallas_call(hand_out, out_shape=(jax.ShapeDtypeStruct((4, nscen), F32)...  1.27 us

profile of v4, /device:TPU:1, one launch (start us, length us, event | category | flops | bytes accessed | tf_op | source)
XLA Modules:
  0.0 42.0 jit_solution(1078133364620536540)
XLA Ops:
  0.6 40.1 %residuals.1 = (f32[8,2,1280]{2,1,0:T(2,128)S(1)}, f32[8,1280]{1,0:T(8,128)S(1)}, f32[8,1664]{1,0:T(8,128)S(1)}, f32[8,128]{1,0:T(8,128)S(1)}, f32[1,128]{1,0:T(1,128)S(1)}) custom-call(f32[1,40]{1,0:T(1,128)} %bitcast.16, f32[1,40]{1,0:T(1,128)} %bitcast.17, s32[13,128]{1,0:T(8,128)} %bitcast.10, s32[13,128]{1,0:T(8,128)} %bitcast.11, f32[13,128]{1,0:T(8,128)} %bitcast.12, ...), custom_call_target="tpu_custom_call" | custom-call | tf_op jit(solution)/shard_map/residuals/pallas_call | solution.py:492
  40.7 1.3 %hand_out.1 = (f32[4,8]{1,0:T(4,128)}, f32[1,4]{1,0:T(1,128)}, f32[8,2,1280]{2,1,0:T(2,128)}, f32[8,1280]{1,0:T(8,128)}, f32[8,1664]{1,0:T(8,128)}) custom-call(f32[8,128]{1,0:T(8,128)S(1)} %get-tuple-element.15.norms, f32[1,128]{1,0:T(1,128)S(1)} %get-tuple-element.16.total, f32[8,2,1280]{2,1,0:T(2,128)S(1)} %get-tuple-element.17.mis, ...), custom_call_target="tpu_custom_call" | custom-call | tf_op jit(solution)/shard_map/hand_out/pallas_call | solution.py:566

commit v5 on v4

--- a/solution.py
+++ b/solution.py
@@ -44,6 +44,7 @@
     status_v,
     slack_v,
     zdual_v,
+    base_s,
     base_v,
     base_z,
     base_all,
@@ -85,24 +86,22 @@
     nline = status.shape[1]
     bus_tiles, line_tiles = nbus // LANES, nline // LANES
 
-    pairs = (
-        (from_bus, lines_i.at[0]),
-        (to_bus, lines_i.at[1]),
-        (mult, mult_v),
-        (delta, delta_v),
-        (conduct, lines_f.at[0]),
-        (suscept, lines_f.at[1]),
-        (charging, lines_f.at[2]),
-        (rating, lines_f.at[3]),
-        (status, status_v),
-        (slack, slack_v),
-        (net, net_v),
-        (ang, ang_v),
-        (zdual, zdual_v),
-    )
-    loads = [pltpu.make_async_copy(a, b, load_sem.at[n]) for n, (a, b) in enumerate(pairs)]
-    for c in loads:
-        c.start()
+    loads = {}
+
+    def load(name, source, place):
+        loads[name] = pltpu.make_async_copy(source, place, load_sem.at[len(loads)])
+        loads[name].start()
+
+    def loaded(*names):
+        for name in names:
+            loads[name].wait()
+
+    load("from", from_bus, lines_i.at[0])
+    load("to", to_bus, lines_i.at[1])
+    load("mult", mult, mult_v)
+    load("vm", base_vm, base_s.at[0])
+    load("va", base_va, base_s.at[1])
+    load("delta", delta, delta_v)
 
     barrier = pltpu.get_barrier_semaphore()
     for d in range(1, ranks):
@@ -113,31 +112,35 @@
         return carry
 
     lax.fori_loop(1, planes, greet, 0)
-    piece = base_vm.shape[1]
-    base_v[0:1, 0:piece] = base_vm[...]
-    base_v[1:2, 0:piece] = base_va[...]
-    for c in loads:
-        c.wait()
+
+    for n, ref in enumerate((conduct, suscept, charging, rating)):
+        load(n, ref, lines_f.at[n])
+    load("status", status, status_v)
+    load("slack", slack, slack_v)
+    load("net", net, net_v)
+    load("ang", ang, ang_v)
+    load("zdual", zdual, zdual_v)
 
     lane8 = lax.broadcasted_iota(I32, (ranks, LANES), 1)
     row8 = lax.broadcasted_iota(I32, (ranks, LANES), 0)
-    comp_sq = jnp.zeros((ranks, LANES), F32)
-    for t in range(line_tiles):
-        cols = slice(t * LANES, (t + 1) * LANES)
-        comp = status_v[:, cols].astype(F32) * (zdual_v[:, cols] * slack_v[:, cols] - 0.01)
-        comp_sq += comp * comp
-    comp_sum = jnp.sum(comp_sq, axis=1, keepdims=True)
-    comp_row = jnp.sum(jnp.where(lane8 == row8 + 8, comp_sum, 0.0), axis=0, keepdims=True)
+    piece = base_vm.shape[0]
+    loaded("vm", "va")
+    for q in range(2):
+        spread_out = jnp.zeros((1, LANES), F32)
+        for n in range(piece):
+            spread_out = jnp.where(lane8[0:1] == n, base_s[q, n], spread_out)
+        base_v[q : q + 1, :] = spread_out
+    loaded("from", "to", "mult")
 
     pl.semaphore_wait(barrier, ranks - 1 + planes - 1)
 
-    half = lambda ref: ref.at[pl.ds(2 * core, 2)]
+    quad = lax.rem(me, 4)
     groups = (
         (lambda s: base_v, lambda r: base_z.at[r], base_z),
         (lambda s: lines_i.at[core], lambda r: idx.at[core, :, r, :], idx.at[core]),
         (lambda s: mult_v.at[s], lambda r: mult_all.at[:, r, :], mult_all),
         (lambda s: delta_v.at[s], lambda r: delta_all.at[:, r, :], delta_all),
-        (lambda s: half(lines_f), lambda r: coef.at[pl.ds(2 * core, 2), :, r, :], half(coef)),
+        (lambda s: lines_f.at[quad], lambda r: coef.at[quad, :, r, :], coef.at[quad]),
         (lambda s: status_v.at[s], lambda r: status_all.at[r], status_all),
         (lambda s: slack_v.at[s], lambda r: slack_all.at[r], slack_all),
         (lambda s: net_v.at[s], lambda r: net_all.at[:, r, :], net_all),
@@ -160,21 +163,21 @@
     def take(n, whole):
         pltpu.make_async_copy(whole, whole, recv_sem.at[n]).wait()
 
-    for n, (source, place, _) in enumerate(groups):
-        send(n, source, place)
-
-    def across(n, mine, theirs):
-        out = pltpu.make_async_remote_copy(
-            src_ref=mine,
-            dst_ref=mine,
-            send_sem=pass_send.at[n],
-            recv_sem=pass_recv.at[n],
-            device_id=(partner, rank),
-            device_id_type=MESH,
-        )
-        out.start()
-        return out, pltpu.make_async_copy(theirs, theirs, pass_recv.at[n])
-
+    needs = {3: ("delta",), 4: (0, 1, 2, 3), 5: ("status",), 6: ("slack",), 7: ("net",), 8: ("ang",)}
+    for n in (0, 1, 2, 4, 3, 5, 6, 7, 8):
+        loaded(*needs.get(n, ()))
+        send(n, *groups[n][:2])
+
+    take(1, idx.at[core])
+    idx_out = pltpu.make_async_remote_copy(
+        src_ref=idx.at[core],
+        dst_ref=idx.at[core],
+        send_sem=pass_send.at[0],
+        recv_sem=pass_recv.at[0],
+        device_id=(partner, rank),
+        device_id_type=MESH,
+    )
+    idx_out.start()
     take(0, base_z)
     group = planes // ranks
     home = base_all.at[lax.rem(me, group), :, :, me // group, :]
@@ -193,10 +196,17 @@
 
     lax.fori_loop(1, planes, spread, 0)
 
-    take(1, idx.at[core])
-    idx_out, idx_in = across(0, idx.at[core], idx.at[1 - core])
+    loaded("zdual")
+    comp_sq = jnp.zeros((ranks, LANES), F32)
+    for t in range(line_tiles):
+        cols = slice(t * LANES, (t + 1) * LANES)
+        comp = status_v[:, cols].astype(F32) * (zdual_v[:, cols] * slack_v[:, cols] - 0.01)
+        comp_sq += comp * comp
+    comp_sum = jnp.sum(comp_sq, axis=1, keepdims=True)
+    comp_row = jnp.sum(jnp.where(lane8 == row8 + 8, comp_sum, 0.0), axis=0, keepdims=True)
+
     take(2, mult_all)
-    idx_in.wait()
+    pltpu.make_async_copy(idx.at[1 - core], idx.at[1 - core], pass_recv.at[0]).wait()
 
     row16 = lax.broadcasted_iota(I32, (16, LANES), 0)
     ramp16 = row16.astype(F32).astype(BF16)
@@ -268,7 +278,19 @@
         by_matmul(k, 2, store)
         return carry
 
-    lax.fori_loop(0, line_tiles, gather_mult, 0, unroll=True)
+    middle = line_tiles // 3
+    lax.fori_loop(0, middle, gather_mult, 0, unroll=True)
+    take(4, coef.at[quad])
+    for d in range(1, 4):
+        pltpu.make_async_remote_copy(
+            src_ref=coef.at[quad],
+            dst_ref=coef.at[quad],
+            send_sem=pass_send.at[1],
+            recv_sem=pass_recv.at[1],
+            device_id=(me - quad + lax.rem(quad + d, 4), rank),
+            device_id_type=MESH,
+        ).start()
+    lax.fori_loop(middle, line_tiles, gather_mult, 0, unroll=True)
 
     take(3, delta_all)
     pltpu.make_async_copy(base_all, base_all, base_recv).wait()
@@ -289,9 +311,6 @@
         if q == 0:
             stack(0, lambda t: tiles[t] - 1.0)
 
-    take(4, half(coef))
-    coef_out, coef_in = across(1, half(coef), coef.at[pl.ds(2 - 2 * core, 2)])
-
     def gather_volt(k, carry):
         def store_vm(e, q, value):
             ends[4 * e, k] = value + 1.0
@@ -305,7 +324,7 @@
 
     lax.fori_loop(0, line_tiles, gather_volt, 0, unroll=True)
 
-    coef_in.wait()
+    pltpu.make_async_copy(coef.at[0:3], coef.at[0:3], pass_recv.at[1]).wait()
     take(5, status_all)
 
     def flows(k, carry):
@@ -428,7 +447,7 @@
     take(n_mis, mismatch)
     take(n_dual, dual)
     idx_out.wait_send()
-    coef_out.wait_send()
+    pltpu.make_async_copy(coef.at[0:3], coef.at[0:3], pass_send.at[1]).wait()
     for n, (_, _, dest) in enumerate(groups):
         sent(send_sem.at[n], dest, ranks)
     for n, dest in ((n_limit, limit), (n_mis, mismatch), (n_dual, dual), (n_sq, sq_all)):
@@ -487,7 +506,6 @@
     V = pltpu.VMEM
     bus, line, deep = (ranks, nbus), (ranks, nline), (tiles, ranks, LANES)
     sem = pltpu.SemaphoreType.DMA
-    row = lambda a: a.reshape(1, -1)
     grid = lambda a: a.reshape(tiles, LANES)
     results = pl.pallas_call(
         functools.partial(kernel, planes, ranks),
@@ -498,7 +516,7 @@
             V((nscen, LANES), F32),
             V((1, LANES), F32),
         ),
-        in_specs=[vmem] * 2 + [hbm] * 13,
+        in_specs=[hbm] * 15,
         out_specs=(vmem,) * 5,
         scratch_shapes=[
             V((2, tiles, LANES), I32),
@@ -510,6 +528,7 @@
             V((nscen, nline), I32),
             V((nscen, nline), F32),
             V((nscen, nline), F32),
+            pltpu.SMEM((2, base_vm.shape[0]), F32),
             V((2, LANES), F32),
             V((ranks, 2, LANES), F32),
             V((planes // ranks, ranks, 2, ranks, LANES), F32),
@@ -533,7 +552,7 @@
             V((ranks, 1, LANES), F32),
             V((1, LANES), F32),
             V((planes, 1, LANES), F32),
-            sem((13,)),
+            sem((15,)),
             sem((13,)),
             sem((13,)),
             sem((2,)),
@@ -546,8 +565,8 @@
         compiler_params=pltpu.CompilerParams(collective_id=0, has_side_effects=True),
         name="residuals",
     )(
-        row(base_vm),
-        row(base_va),
+        base_vm,
+        base_va,
         grid(from_bus),
         grid(to_bus),
         grid(conduct),

time: 42.1 us -> 40.7 us (0.967)
  Pallas kernels: 41.3 us -> 39.9 us
    pallas_call x1, Pallas kernels: 40.1 us -> 38.7 us  [per_device(): pl.pallas_call(functools.partial(kernel, planes, ranks), out_shape=(V((ns...]
where the time goes in v5:
time: 40.7 us; the launch traced here: 40.6 us
  Pallas kernels  39.9 us (98%)
  between operations  0.65 us (2%)
    pallas_call x1, Pallas kernels, per_device(): pl.pallas_call(functools.partial(kernel, planes, ranks), out_shape=(V((ns...  38.7 us
    pallas_call x1, Pallas kernels, per_device(): pl.pallas_call(hand_out, out_shape=(jax.ShapeDtypeStruct((4, nscen), F32)...  1.27 us

profile of v5, /device:TPU:1, one launch (start us, length us, event | category | flops | bytes accessed | tf_op | source)
XLA Modules:
  0.0 40.6 jit_solution(11367694125996940603)
XLA Ops:
  0.6 38.7 %residuals.1 = (f32[8,2,1280]{2,1,0:T(2,128)S(1)}, f32[8,1280]{1,0:T(8,128)S(1)}, f32[8,1664]{1,0:T(8,128)S(1)}, f32[8,128]{1,0:T(8,128)S(1)}, f32[1,128]{1,0:T(1,128)S(1)}) custom-call(f32[40]{0:T(128)} %base_vm.1, f32[40]{0:T(128)} %base_va.1, s32[13,128]{1,0:T(8,128)} %bitcast.8, s32[13,128]{1,0:T(8,128)} %bitcast.9, f32[13,128]{1,0:T(8,128)} %bitcast.10, ...), custom_call_target="tpu_custom_call" | custom-call | tf_op jit(solution)/shard_map/residuals/pallas_call | solution.py:510
  39.3 1.3 %hand_out.1 = (f32[4,8]{1,0:T(4,128)}, f32[1,4]{1,0:T(1,128)}, f32[8,2,1280]{2,1,0:T(2,128)}, f32[8,1280]{1,0:T(8,128)}, f32[8,1664]{1,0:T(8,128)}) custom-call(f32[8,128]{1,0:T(8,128)S(1)} %get-tuple-element.15.norms, f32[1,128]{1,0:T(1,128)S(1)} %get-tuple-element.16.total, f32[8,2,1280]{2,1,0:T(2,128)S(1)} %get-tuple-element.17.mis, ...), custom_call_target="tpu_custom_call" | custom-call | tf_op jit(solution)/shard_map/hand_out/pallas_call | solution.py:585

commit v6 on v5

--- a/solution.py
+++ b/solution.py
@@ -311,23 +311,37 @@
         if q == 0:
             stack(0, lambda t: tiles[t] - 1.0)
 
-    def gather_volt(k, carry):
-        def store_vm(e, q, value):
+    def gather_angle(k):
+        def store(e, value):
+            ends[4 * e + 1, k] = value
+
+        by_permute(k, store)
+
+    def gather_size(k):
+        def store(e, q, value):
             ends[4 * e, k] = value + 1.0
 
-        def store_va(e, value):
-            ends[4 * e + 1, k] = value
-
-        by_permute(k, store_va)
-        by_matmul(k, 1, store_vm)
-        return carry
-
-    lax.fori_loop(0, line_tiles, gather_volt, 0, unroll=True)
+        by_matmul(k, 1, store)
+
+    late = 4
+    early = line_tiles - late
+
+    def gather_both(k, carry):
+        gather_angle(k)
+        gather_size(k)
+        return carry
+
+    def gather_rest(k, carry):
+        gather_size(k)
+        return carry
+
+    lax.fori_loop(0, early, gather_both, 0, unroll=True)
+    lax.fori_loop(early, line_tiles, gather_rest, 0, unroll=True)
 
     pltpu.make_async_copy(coef.at[0:3], coef.at[0:3], pass_recv.at[1]).wait()
     take(5, status_all)
 
-    def flows(k, carry):
+    def flows(k):
         cols = pl.ds(pl.multiple_of(k * LANES, LANES), LANES)
         vf, af, mpf, mqf = (ends[q, k] for q in range(4))
         vt, at, mpt, mqt = (ends[4 + q, k] for q in range(4))
@@ -344,28 +358,12 @@
         fd = u * (mpf * (gsn - bcs) - mqf * (gcs + bsn) + mpt * (gsn + bcs) + mqt * (gcs - bsn)) * live
         for n, v in enumerate((pf, qf, fd, pt, qt, -fd)):
             terms[n, k] = v
-        return carry
-
-    lax.fori_loop(0, line_tiles, flows, 0, unroll=True)
-
-    take(6, slack_all)
-    limit_sq = jnp.zeros((ranks, LANES), F32)
-    for k in range(line_tiles):
-        cols = slice(k * LANES, (k + 1) * LANES)
-        pf, qf = terms[0, k], terms[1, k]
-        live = status_all[:, cols].astype(F32)
-        lim = live * (pf * pf + qf * qf + slack_all[:, cols] - coef[3, k] * coef[3, k])
-        limit_out[:, cols] = lim
-        limit_sq += lim * lim
-
-    n_limit, n_mis, n_dual, n_sq = (len(groups) + n for n in range(4))
-    send(n_limit, lambda s: limit_out.at[s], lambda r: limit.at[r])
 
     per = nbus // 256
     high_of = [((row16 & 7) * per + j).astype(F32).astype(BF16) for j in range(per)]
     sums[...] = jnp.zeros_like(sums)
 
-    def scatter(k, carry):
+    def scatter(k):
         for s in range(ranks):
             left, right = [], []
             for e in range(2):
@@ -393,9 +391,30 @@
                 (((1,), (1,)), ((), ())),
                 preferred_element_type=F32,
             )
-        return carry
-
-    lax.fori_loop(0, line_tiles, scatter, 0, unroll=True)
+
+    def first_steps(k, carry):
+        gather_angle(k + early)
+        flows(k)
+        scatter(k)
+        return carry
+
+    def other_steps(k, carry):
+        flows(k)
+        scatter(k)
+        return carry
+
+    lax.fori_loop(0, late, first_steps, 0, unroll=True)
+    lax.fori_loop(late, line_tiles, other_steps, 0, unroll=True)
+
+    take(6, slack_all)
+    limit_sq = jnp.zeros((ranks, LANES), F32)
+    for k in range(line_tiles):
+        cols = slice(k * LANES, (k + 1) * LANES)
+        pf, qf = terms[0, k], terms[1, k]
+        live = status_all[:, cols].astype(F32)
+        lim = live * (pf * pf + qf * qf + slack_all[:, cols] - coef[3, k] * coef[3, k])
+        limit_out[:, cols] = lim
+        limit_sq += lim * lim
 
     take(7, net_all)
     take(8, ang_all)
@@ -418,16 +437,16 @@
     for n, part in enumerate((mis_sq, dual_sq, limit_sq)):
         mine = jnp.where(lane8[0:1] == n, jnp.sum(part, keepdims=True), mine)
     sq_mine[...] = mine
+    n_limit, n_mis, n_dual, n_sq = (len(groups) + n for n in range(4))
     send(n_sq, lambda s: sq_mine, lambda r: sq_all.at[r])
     send(n_mis, lambda s: mis_out.at[:, s, :], lambda r: mismatch.at[r])
     send(n_dual, lambda s: dual_out.at[s], lambda r: dual.at[r])
+    send(n_limit, lambda s: limit_out.at[s], lambda r: limit.at[r])
 
     take(n_sq, sq_all)
     every = sq_all[:, 0, :]
-    comp_all = jnp.sum(every, axis=0, keepdims=True)
-    comp_of = jnp.sum(jnp.where(lane8 == row8 + 8, comp_all, 0.0), axis=1, keepdims=True)
-    squares = jnp.where(lane8 == 3, comp_of, jnp.where(lane8 < 3, every, 0.0))
-    tot_mine[...] = jnp.sum(squares, axis=0, keepdims=True)
+    group_sum = jnp.sum(every, axis=0, keepdims=True)
+    tot_mine[...] = group_sum
     pltpu.make_async_copy(tot_mine, tot_all.at[me], tot_recv).start()
 
     def share(d, carry):
@@ -442,7 +461,8 @@
         return carry
 
     lax.fori_loop(1, planes, share, 0)
-    norms[...] = jnp.sqrt(squares)
+    comp_of = jnp.sum(jnp.where(lane8 == row8 + 8, group_sum, 0.0), axis=1, keepdims=True)
+    norms[...] = jnp.sqrt(jnp.where(lane8 == 3, comp_of, jnp.where(lane8 < 3, every, 0.0)))
     take(n_limit, limit)
     take(n_mis, mismatch)
     take(n_dual, dual)
@@ -458,6 +478,9 @@
     pltpu.make_async_copy(part, part, base_send).wait()
     pltpu.make_async_copy(tot_all, tot_all, tot_recv).wait()
     whole = jnp.sum(tot_all[:, 0, :], axis=0, keepdims=True)
+    lane1 = lane8[0:1]
+    comp_whole = jnp.sum(jnp.where((lane1 >= 8) & (lane1 < 8 + ranks), whole, 0.0), axis=1, keepdims=True)
+    whole = jnp.where(lane1 == 3, comp_whole, jnp.where(lane1 < 3, whole, 0.0))
     total[...] = jnp.sqrt(whole / (planes * ranks))
     part = tot_all.at[0 : planes - 1]
     pltpu.make_async_copy(part, part, tot_send).wait()

time: 40.7 us -> 39.9 us (0.980)
  Pallas kernels: 39.9 us -> 39.2 us
    pallas_call x1, Pallas kernels: 38.7 us -> 37.9 us  [per_device(): pl.pallas_call(functools.partial(kernel, planes, ranks), out_shape=(V((ns...]
where the time goes in v6:
time: 39.9 us; the launch traced here: 39.8 us
  Pallas kernels  39.2 us (98%)
  between operations  0.65 us (2%)
    pallas_call x1, Pallas kernels, per_device(): pl.pallas_call(functools.partial(kernel, planes, ranks), out_shape=(V((ns...  37.9 us
    pallas_call x1, Pallas kernels, per_device(): pl.pallas_call(hand_out, out_shape=(jax.ShapeDtypeStruct((4, nscen), F32)...  1.27 us

profile of v6, /device:TPU:1, one launch (start us, length us, event | category | flops | bytes accessed | tf_op | source)
XLA Modules:
  0.0 39.8 jit_solution(13078848095306151806)
XLA Ops:
  0.6 37.9 %residuals.1 = (f32[8,2,1280]{2,1,0:T(2,128)S(1)}, f32[8,1280]{1,0:T(8,128)S(1)}, f32[8,1664]{1,0:T(8,128)S(1)}, f32[8,128]{1,0:T(8,128)S(1)}, f32[1,128]{1,0:T(1,128)S(1)}) custom-call(f32[40]{0:T(128)} %base_vm.1, f32[40]{0:T(128)} %base_va.1, s32[13,128]{1,0:T(8,128)} %bitcast.8, s32[13,128]{1,0:T(8,128)} %bitcast.9, f32[13,128]{1,0:T(8,128)} %bitcast.10, ...), custom_call_target="tpu_custom_call" | custom-call | tf_op jit(solution)/shard_map/residuals/pallas_call | solution.py:533
  38.6 1.3 %hand_out.1 = (f32[4,8]{1,0:T(4,128)}, f32[1,4]{1,0:T(1,128)}, f32[8,2,1280]{2,1,0:T(2,128)}, f32[8,1280]{1,0:T(8,128)}, f32[8,1664]{1,0:T(8,128)}) custom-call(f32[8,128]{1,0:T(8,128)S(1)} %get-tuple-element.15.norms, f32[1,128]{1,0:T(1,128)S(1)} %get-tuple-element.16.total, f32[8,2,1280]{2,1,0:T(2,128)S(1)} %get-tuple-element.17.mis, ...), custom_call_target="tpu_custom_call" | custom-call | tf_op jit(solution)/shard_map/hand_out/pallas_call | solution.py:608

commit v7 on v6

--- a/solution.py
+++ b/solution.py
@@ -149,7 +149,7 @@
 
     def send(n, source, place):
         pltpu.make_async_copy(source(rank), place(rank), recv_sem.at[n]).start()
-        for d in range(1, ranks):
+        for d in (4, 3, 5, 2, 6, 1, 7):
             peer = lax.rem(rank + d, ranks)
             pltpu.make_async_remote_copy(
                 src_ref=source(peer),
@@ -492,15 +492,12 @@
     pltpu.make_async_copy(part, part, sem).wait()
 
 
-def hand_out(norms, total, mis, dual, limit, norms_out, total_out, mis_out, dual_out, limit_out, sem):
-    pairs = ((mis, mis_out), (dual, dual_out), (limit, limit_out))
-    copies = [pltpu.make_async_copy(a, b, sem.at[n]) for n, (a, b) in enumerate(pairs)]
-    for c in copies:
-        c.start()
+def hand_out(norms, total, mis, dual, limit, norms_out, total_out, mis_out, dual_out, limit_out):
+    mis_out[...] = mis[...]
+    dual_out[...] = dual[...]
+    limit_out[...] = limit[...]
     norms_out[...] = norms[...].T[0:4, :]
     total_out[...] = total[:, 0:4]
-    for c in copies:
-        c.wait()
 
 
 def per_device(
@@ -615,8 +612,7 @@
             jax.ShapeDtypeStruct((nscen, nline), F32),
         ),
         in_specs=[vmem] * 5,
-        out_specs=(vmem, vmem, hbm, hbm, hbm),
-        scratch_shapes=[sem((3,))],
+        out_specs=(vmem,) * 5,
         name="hand_out",
     )(norms, total, mis, dual, limit)
     return mis, dual, limit, norms.T, total.reshape(4)

time: 39.9 us -> 39.1 us (0.980)
  Pallas kernels: 39.2 us -> 38.4 us
    pallas_call x1, Pallas kernels: 1.27 us -> 0.67 us  [per_device(): pl.pallas_call(hand_out, out_shape=(jax.ShapeDtypeStruct((4, nscen), F32)...]
where the time goes in v7:
time: 39.1 us; the launch traced here: 39 us
  Pallas kernels  38.4 us (98%)
  between operations  0.65 us (2%)
    pallas_call x1, Pallas kernels, per_device(): pl.pallas_call(functools.partial(kernel, planes, ranks), out_shape=(V((ns...  37.7 us

profile of v7, /device:TPU:1, one launch (start us, length us, event | category | flops | bytes accessed | tf_op | source)
XLA Modules:
  0.0 39.0 jit_solution(1184542167694423891)
XLA Ops:
  0.6 37.7 %residuals.1 = (f32[8,2,1280]{2,1,0:T(2,128)S(1)}, f32[8,1280]{1,0:T(8,128)S(1)}, f32[8,1664]{1,0:T(8,128)S(1)}, f32[8,128]{1,0:T(8,128)S(1)}, f32[1,128]{1,0:T(1,128)S(1)}) custom-call(f32[40]{0:T(128)} %base_vm.1, f32[40]{0:T(128)} %base_va.1, s32[13,128]{1,0:T(8,128)} %bitcast.8, s32[13,128]{1,0:T(8,128)} %bitcast.9, f32[13,128]{1,0:T(8,128)} %bitcast.10, ...), custom_call_target="tpu_custom_call" | custom-call | tf_op jit(solution)/shard_map/residuals/pallas_call | solution.py:530
  38.3 0.7 %hand_out.1 = (f32[4,8]{1,0:T(4,128)}, f32[1,4]{1,0:T(1,128)}, f32[8,2,1280]{2,1,0:T(2,128)}, f32[8,1280]{1,0:T(8,128)}, f32[8,1664]{1,0:T(8,128)}) custom-call(f32[8,128]{1,0:T(8,128)S(1)} %get-tuple-element.15.norms, f32[1,128]{1,0:T(1,128)S(1)} %get-tuple-element.16.total, f32[8,2,1280]{2,1,0:T(2,128)S(1)} %get-tuple-element.17.mis, ...), custom_call_target="tpu_custom_call" | custom-call | tf_op jit(solution)/shard_map/hand_out/pallas_call | solution.py:605

commit v8 on v7

--- a/solution.py
+++ b/solution.py
@@ -323,7 +323,7 @@
 
         by_matmul(k, 1, store)
 
-    late = 4
+    late = 6
     early = line_tiles - late
 
     def gather_both(k, carry):

time: 39.1 us -> 39.2 us (level)
  no operation moved by 1% of the time
where the time goes in v8:
time: 39.2 us; the launch traced here: 39 us
  Pallas kernels  38.4 us (98%)
  between operations  0.65 us (2%)
    pallas_call x1, Pallas kernels, per_device(): pl.pallas_call(functools.partial(kernel, planes, ranks), out_shape=(V((ns...  37.7 us

profile of v8, /device:TPU:1, one launch (start us, length us, event | category | flops | bytes accessed | tf_op | source)
XLA Modules:
  0.0 39.0 jit_solution(17950889565366286743)
XLA Ops:
  0.6 37.7 %residuals.1 = (f32[8,2,1280]{2,1,0:T(2,128)S(1)}, f32[8,1280]{1,0:T(8,128)S(1)}, f32[8,1664]{1,0:T(8,128)S(1)}, f32[8,128]{1,0:T(8,128)S(1)}, f32[1,128]{1,0:T(1,128)S(1)}) custom-call(f32[40]{0:T(128)} %base_vm.1, f32[40]{0:T(128)} %base_va.1, s32[13,128]{1,0:T(8,128)} %bitcast.8, s32[13,128]{1,0:T(8,128)} %bitcast.9, f32[13,128]{1,0:T(8,128)} %bitcast.10, ...), custom_call_target="tpu_custom_call" | custom-call | tf_op jit(solution)/shard_map/residuals/pallas_call | solution.py:530
  38.4 0.7 %hand_out.1 = (f32[4,8]{1,0:T(4,128)}, f32[1,4]{1,0:T(1,128)}, f32[8,2,1280]{2,1,0:T(2,128)}, f32[8,1280]{1,0:T(8,128)}, f32[8,1664]{1,0:T(8,128)}) custom-call(f32[8,128]{1,0:T(8,128)S(1)} %get-tuple-element.15.norms, f32[1,128]{1,0:T(1,128)S(1)} %get-tuple-element.16.total, f32[8,2,1280]{2,1,0:T(2,128)S(1)} %get-tuple-element.17.mis, ...), custom_call_target="tpu_custom_call" | custom-call | tf_op jit(solution)/shard_map/hand_out/pallas_call | solution.py:605
